TPU v7x, 16 devices: a whole 2x2x2 slice. The times are simulated.
16 devices in a mesh: fsdp: 2 (over z), model: 8 (over y, x, core).
Axes of the slice: x: 2, y: 2, z: 2, core: 2. Of those that a mesh axis runs over, the one named last changes fastest.
Arguments:
- x_in: bfloat16 [16, 256, 5120], P('fsdp', 'model')
- gain_attn: float32 [2, 5120], replicated
- gain_mlp: float32 [2, 5120], replicated
- rope_cos: float32 [256, 64], replicated
- rope_sin: float32 [256, 64], replicated
- w_q: bfloat16 [2, 5120, 5120], P(None, 'fsdp', 'model')
- w_k: bfloat16 [2, 5120, 1024], P(None, 'fsdp', 'model')
- w_v: bfloat16 [2, 5120, 1024], P(None, 'fsdp', 'model')
- w_o: bfloat16 [2, 5120, 5120], P(None, 'model', 'fsdp')
- w_gate: bfloat16 [2, 5120, 13824], P(None, 'fsdp', 'model')
- w_up: bfloat16 [2, 5120, 13824], P(None, 'fsdp', 'model')
- w_down: bfloat16 [2, 13824, 5120], P(None, 'model', 'fsdp')
Outputs:
- output: bfloat16 [16, 256, 5120], P('fsdp', 'model')
All inputs are finite; a program needn't handle non-finite values.
Results may differ from a plain program's by a relative error of at most 0.02.
Values are sent between devices in bfloat16 or wider.
A program may use at most 1 GiB of HBM per device.

v0:
```python
import jax
import jax.numpy as jnp
from jax import lax
from jax.sharding import PartitionSpec as P

EPS = 1e-5


def rms_norm(seq_rows, gain_vec):
    rows_f = seq_rows.astype(jnp.float32)
    mean_sq = jnp.mean(rows_f * rows_f, axis=-1, keepdims=True)
    return (rows_f * lax.rsqrt(mean_sq + EPS) * gain_vec).astype(jnp.bfloat16)


def rotate(head_vals, cos_b, sin_b):
    half_dim = head_vals.shape[-1] // 2
    heads_f = head_vals.astype(jnp.float32)
    first_half = heads_f[..., :half_dim]
    second_half = heads_f[..., half_dim:]
    return jnp.concatenate([first_half * cos_b - second_half * sin_b, second_half * cos_b + first_half * sin_b], axis=-1).astype(jnp.bfloat16)


def attend(q_proj, k_proj, v_proj, rope_cos, rope_sin, kv_count):
    batch_rows, seq_len, q_width = q_proj.shape
    head_dim = 2 * rope_cos.shape[1]
    group_size = q_width // (head_dim * kv_count)
    q_rot = rotate(q_proj.reshape(batch_rows, seq_len, kv_count, group_size, head_dim), rope_cos[None, :, None, None, :], rope_sin[None, :, None, None, :])
    k_rot = rotate(k_proj.reshape(batch_rows, seq_len, kv_count, head_dim), rope_cos[None, :, None, :], rope_sin[None, :, None, :])
    v_heads = v_proj.reshape(batch_rows, seq_len, kv_count, head_dim)
    scores = jnp.einsum('bqkgd,bskd->bkgqs', q_rot, k_rot, preferred_element_type=jnp.float32) * head_dim ** -0.5
    positions = jnp.arange(seq_len)
    causal = positions[:, None] >= positions[None, :]
    scores = jnp.where(causal, scores, -jnp.inf)
    attn_probs = jax.nn.softmax(scores, axis=-1).astype(jnp.bfloat16)
    attn_out = jnp.einsum('bkgqs,bskd->bqkgd', attn_probs, v_heads, preferred_element_type=jnp.float32).astype(jnp.bfloat16)
    return attn_out.reshape(batch_rows, seq_len, q_width)


def solution(mesh):
    act_spec = P('fsdp', 'model', None)
    col_spec = P(None, 'fsdp', 'model')
    row_spec = P(None, 'model', 'fsdp')

    def device_step(x_in, gain_attn, gain_mlp, rope_cos, rope_sin, w_q, w_k, w_v, w_o, w_gate, w_up, w_down):
        head_dim = 2 * rope_cos.shape[1]
        kv_local = w_k.shape[-1] // head_dim
        residual = x_in
        for layer_idx in range(w_q.shape[0]):
            wq_full = lax.all_gather(w_q[layer_idx], 'fsdp', axis=0, tiled=True)
            wk_full = lax.all_gather(w_k[layer_idx], 'fsdp', axis=0, tiled=True)
            wv_full = lax.all_gather(w_v[layer_idx], 'fsdp', axis=0, tiled=True)
            wo_full = lax.all_gather(w_o[layer_idx], 'fsdp', axis=1, tiled=True)
            normed = rms_norm(residual, gain_attn[layer_idx])
            normed_all = lax.all_gather(normed, 'model', axis=1, tiled=True)
            q_proj = jnp.einsum('bsd,dn->bsn', normed_all, wq_full, preferred_element_type=jnp.float32).astype(jnp.bfloat16)
            k_proj = jnp.einsum('bsd,dn->bsn', normed_all, wk_full, preferred_element_type=jnp.float32).astype(jnp.bfloat16)
            v_proj = jnp.einsum('bsd,dn->bsn', normed_all, wv_full, preferred_element_type=jnp.float32).astype(jnp.bfloat16)
            attn_out = attend(q_proj, k_proj, v_proj, rope_cos, rope_sin, kv_local)
            attn_part = jnp.einsum('bsn,nd->bsd', attn_out, wo_full, preferred_element_type=jnp.float32)
            attn_sum = lax.psum_scatter(attn_part, 'model', scatter_dimension=1, tiled=True)
            mid_rows = (residual.astype(jnp.float32) + attn_sum).astype(jnp.bfloat16)
            wg_full = lax.all_gather(w_gate[layer_idx], 'fsdp', axis=0, tiled=True)
            wu_full = lax.all_gather(w_up[layer_idx], 'fsdp', axis=0, tiled=True)
            wd_full = lax.all_gather(w_down[layer_idx], 'fsdp', axis=1, tiled=True)
            normed_mlp = rms_norm(mid_rows, gain_mlp[layer_idx])
            mlp_in = lax.all_gather(normed_mlp, 'model', axis=1, tiled=True)
            gate_acc = jnp.einsum('bsd,df->bsf', mlp_in, wg_full, preferred_element_type=jnp.float32)
            up_acc = jnp.einsum('bsd,df->bsf', mlp_in, wu_full, preferred_element_type=jnp.float32)
            hidden = (jax.nn.silu(gate_acc) * up_acc).astype(jnp.bfloat16)
            mlp_part = jnp.einsum('bsf,fd->bsd', hidden, wd_full, preferred_element_type=jnp.float32)
            mlp_sum = lax.psum_scatter(mlp_part, 'model', scatter_dimension=1, tiled=True)
            residual = (mid_rows.astype(jnp.float32) + mlp_sum).astype(jnp.bfloat16)
        return residual

    return jax.shard_map(device_step, mesh=mesh, in_specs=(act_spec, P(), P(), P(), P(), col_spec, col_spec, col_spec, row_spec, col_spec, col_spec, row_spec), out_specs=act_spec, check_vma=False)
```

profile of v0, /device:TPU:0, one launch (start us, length us, event | category | flops | bytes accessed | tf_op | source)
XLA Modules:
  0.0 3254.8 jit_solution(17788315073335243749)
XLA Ops:
  29.0 69.0 %all-gather.45.cloned.1.call-done = bf16[1,5120,640]{2,1,0:T(8,128)(2,1)} async-done(((bf16[1,2560,640]{2,1,0:T(8,128)(2,1)}), bf16[1,5120,640]{2,1,0:T(8,128)(2,1)}) %all-gather.45.cloned.1.call-update) | async-done | bytes 6553616 | tf_op jit(solution)/shard_map/all_gather | solution.py:49
  98.0 105.6 %all-gather.33.cloned.1.call-done = bf16[8,256,5120]{2,1,0:T(8,128)(2,1)} async-done(((bf16[8,32,5120]{2,1,0:T(8,128)(2,1)}), bf16[8,256,5120]{2,1,0:T(8,128)(2,1)}) %all-gather.33.cloned.1.call-update) | async-done | bytes 20971536 | tf_op jit(solution)/shard_map/all_gather | solution.py:54
  203.6 22.4 convert_convert_fusion.1
  247.5 12.1 fusion.102
  271.1 23.9 fusion.60
  295.0 39.1 %all-gather.47.cloned.1.call-done = bf16[1,640,5120]{2,1,0:T(8,128)(2,1)} async-done(((bf16[1,640,2560]{2,1,0:T(8,128)(2,1)}), bf16[1,640,5120]{2,1,0:T(8,128)(2,1)}) %all-gather.47.cloned.1.call-update) | async-done | bytes 6553616 | tf_op jit(solution)/shard_map/all_gather | solution.py:52
  334.2 26.8 fusion.22
  374.3 225.2 %reduce-scatter.5.cloned.1.call-done = f32[8,32,5120]{2,1,0:T(8,128)} async-done(((f32[8,256,5120]{2,1,0:T(8,128)}), f32[8,32,5120]{2,1,0:T(8,128)}) %reduce-scatter.5.cloned.1.call-update) | async-done | bytes 5242896 | tf_op jit(solution)/shard_map/reduce_scatter | solution.py:60
  618.8 12.0 fusion.133
  630.8 180.2 %all-gather.49.cloned.1.call-done = bf16[1,5120,1728]{1,2,0:T(8,128)(2,1)} async-done(((bf16[1,2560,1728]{1,2,0:T(8,128)(2,1)}), bf16[1,5120,1728]{1,2,0:T(8,128)(2,1)}) %all-gather.49.cloned.1.call-update) | async-done | bytes 17694736 | tf_op jit(solution)/shard_map/all_gather | solution.py:62
  811.0 105.6 %all-gather.35.cloned.1.call-done = bf16[8,256,5120]{2,1,0:T(8,128)(2,1)} async-done(((bf16[8,32,5120]{2,1,0:T(8,128)(2,1)}), bf16[8,256,5120]{2,1,0:T(8,128)(2,1)}) %all-gather.35.cloned.1.call-update) | async-done | bytes 20971536 | tf_op jit(solution)/shard_map/all_gather | solution.py:66
  916.5 45.8 %fusion.10 = f32[8,256,1728]{1,2,0:T(8,128)} fusion(bf16[8,256,5120]{2,1,0:T(8,128)(2,1)} %all-gather.35.cloned.1.call-done, bf16[1,5120,1728]{1,2,0:T(8,128)(2,1)} %all-gather.49.cloned.1.call-done), kind=kOutput, calls=%fused_computation.10 | convolution fusion | flops 36238786560 | bytes 52822016 | tf_op jit(solution)/shard_map/bsd,df->bsf/dot_general | solution.py:67
  962.3 165.7 %all-gather.51.cloned.1.call-done = bf16[1,5120,1728]{1,2,0:T(8,128)(2,1)} async-done(((bf16[1,2560,1728]{1,2,0:T(8,128)(2,1)}), bf16[1,5120,1728]{1,2,0:T(8,128)(2,1)}) %all-gather.51.cloned.1.call-update) | async-done | bytes 17694736 | tf_op jit(solution)/shard_map/all_gather | solution.py:63
  1128.0 45.8 %fusion.8 = f32[8,256,1728]{1,2,0:T(8,128)} fusion(bf16[8,256,5120]{2,1,0:T(8,128)(2,1)} %all-gather.35.cloned.1.call-done, bf16[1,5120,1728]{1,2,0:T(8,128)(2,1)} %all-gather.51.cloned.1.call-done), kind=kOutput, calls=%fused_computation.8 | convolution fusion | flops 36238786560 | bytes 52822016 | tf_op jit(solution)/shard_map/bsd,df->bsf/dot_general | solution.py:68
  1173.8 165.5 %all-gather.53.cloned.1.call-done = bf16[1,1728,5120]{2,1,0:T(8,128)(2,1)} async-done(((bf16[1,1728,2560]{2,1,0:T(8,128)(2,1)}), bf16[1,1728,5120]{2,1,0:T(8,128)(2,1)}) %all-gather.53.cloned.1.call-update) | async-done | bytes 17694736 | tf_op jit(solution)/shard_map/all_gather | solution.py:64
  1339.3 51.1 %fusion.6 = f32[8,256,5120]{2,1,0:T(8,128)} fusion(bf16[1,1728,5120]{2,1,0:T(8,128)(2,1)} %all-gather.53.cloned.1.call-done, f32[8,256,1728]{1,2,0:T(8,128)} %fusion.8, f32[8,256,1728]{1,2,0:T(8,128)} %fusion.10), kind=kOutput, calls=%fused_computation.6 | convolution fusion | flops 36260020224 | bytes 87949312 | tf_op jit(solution)/shard_map/bsf,fd->bsd/dot_general | solution.py:70
  1391.1 237.9 %reduce-scatter.7.cloned.1.call-done = f32[8,32,5120]{2,1,0:T(8,128)} async-done(((f32[8,256,5120]{2,1,0:T(8,128)}), f32[8,32,5120]{2,1,0:T(8,128)}) %reduce-scatter.7.cloned.1.call-update) | async-done | bytes 5242896 | tf_op jit(solution)/shard_map/reduce_scatter | solution.py:71
  1638.1 74.5 %all-gather.59.cloned.1.call-done = bf16[1,5120,640]{2,1,0:T(8,128)(2,1)} async-done(((bf16[1,2560,640]{2,1,0:T(8,128)(2,1)}), bf16[1,5120,640]{2,1,0:T(8,128)(2,1)}) %all-gather.59.cloned.1.call-update) | async-done | bytes 6553616 | tf_op jit(solution)/shard_map/all_gather | solution.py:49
  1712.5 105.6 %all-gather.37.cloned.1.call-done = bf16[8,256,5120]{2,1,0:T(8,128)(2,1)} async-done(((bf16[8,32,5120]{2,1,0:T(8,128)(2,1)}), bf16[8,256,5120]{2,1,0:T(8,128)(2,1)}) %all-gather.37.cloned.1.call-update) | async-done | bytes 20971536 | tf_op jit(solution)/shard_map/all_gather | solution.py:54
  1818.1 22.6 convert_convert_fusion
  1885.6 23.9 fusion.63
  1909.5 39.0 %all-gather.61.cloned.1.call-done = bf16[1,640,5120]{2,1,0:T(8,128)(2,1)} async-done(((bf16[1,640,2560]{2,1,0:T(8,128)(2,1)}), bf16[1,640,5120]{2,1,0:T(8,128)(2,1)}) %all-gather.61.cloned.1.call-update) | async-done | bytes 6553616 | tf_op jit(solution)/shard_map/all_gather | solution.py:52
  1948.5 26.8 fusion.18
  1976.0 237.9 %reduce-scatter.9.cloned.1.call-done = f32[8,32,5120]{2,1,0:T(8,128)} async-done(((f32[8,256,5120]{2,1,0:T(8,128)}), f32[8,32,5120]{2,1,0:T(8,128)}) %reduce-scatter.9.cloned.1.call-update) | async-done | bytes 5242896 | tf_op jit(solution)/shard_map/reduce_scatter | solution.py:60
  2222.6 202.6 %all-gather.63.cloned.1.call-done = bf16[1,5120,1728]{1,2,0:T(8,128)(2,1)} async-done(((bf16[1,2560,1728]{1,2,0:T(8,128)(2,1)}), bf16[1,5120,1728]{1,2,0:T(8,128)(2,1)}) %all-gather.63.cloned.1.call-update) | async-done | bytes 17694736 | tf_op jit(solution)/shard_map/all_gather | solution.py:62
  2425.3 105.6 %all-gather.39.cloned.1.call-done = bf16[8,256,5120]{2,1,0:T(8,128)(2,1)} async-done(((bf16[8,32,5120]{2,1,0:T(8,128)(2,1)}), bf16[8,256,5120]{2,1,0:T(8,128)(2,1)}) %all-gather.39.cloned.1.call-update) | async-done | bytes 20971536 | tf_op jit(solution)/shard_map/all_gather | solution.py:66
  2530.8 46.0 %fusion.4 = f32[8,256,1728]{1,2,0:T(8,128)} fusion(bf16[8,256,5120]{2,1,0:T(8,128)(2,1)} %all-gather.39.cloned.1.call-done, bf16[1,5120,1728]{1,2,0:T(8,128)(2,1)} %all-gather.63.cloned.1.call-done), kind=kOutput, calls=%fused_computation.4 | convolution fusion | flops 36238786560 | bytes 52822016 | tf_op jit(solution)/shard_map/bsd,df->bsf/dot_general | solution.py:67
  2576.9 165.3 %all-gather.65.cloned.1.call-done = bf16[1,5120,1728]{1,2,0:T(8,128)(2,1)} async-done(((bf16[1,2560,1728]{1,2,0:T(8,128)(2,1)}), bf16[1,5120,1728]{1,2,0:T(8,128)(2,1)}) %all-gather.65.cloned.1.call-update) | async-done | bytes 17694736 | tf_op jit(solution)/shard_map/all_gather | solution.py:63
  2742.1 45.7 %fusion.2 = f32[8,256,1728]{1,2,0:T(8,128)} fusion(bf16[8,256,5120]{2,1,0:T(8,128)(2,1)} %all-gather.39.cloned.1.call-done, bf16[1,5120,1728]{1,2,0:T(8,128)(2,1)} %all-gather.65.cloned.1.call-done), kind=kOutput, calls=%fused_computation.2 | convolution fusion | flops 36238786560 | bytes 52822016 | tf_op jit(solution)/shard_map/bsd,df->bsf/dot_general | solution.py:68
  2787.9 165.7 %all-gather.67.cloned.1.call-done = bf16[1,1728,5120]{2,1,0:T(8,128)(2,1)} async-done(((bf16[1,1728,2560]{2,1,0:T(8,128)(2,1)}), bf16[1,1728,5120]{2,1,0:T(8,128)(2,1)}) %all-gather.67.cloned.1.call-update) | async-done | bytes 17694736 | tf_op jit(solution)/shard_map/all_gather | solution.py:64
  2953.6 50.9 %fusion = f32[8,256,5120]{2,1,0:T(8,128)} fusion(bf16[1,1728,5120]{2,1,0:T(8,128)(2,1)} %all-gather.67.cloned.1.call-done, f32[8,256,1728]{1,2,0:T(8,128)} %fusion.2, f32[8,256,1728]{1,2,0:T(8,128)} %fusion.4), kind=kOutput, calls=%fused_computation | convolution fusion | flops 36260020224 | bytes 87949312 | tf_op jit(solution)/shard_map/bsf,fd->bsd/dot_general | solution.py:70
  3004.5 238.6 %reduce-scatter.11.cloned.1.call-done = f32[8,32,5120]{2,1,0:T(8,128)} async-done(((f32[8,256,5120]{2,1,0:T(8,128)}), f32[8,32,5120]{2,1,0:T(8,128)}) %reduce-scatter.11.cloned.1.call-update) | async-done | bytes 5242896 | tf_op jit(solution)/shard_map/reduce_scatter | solution.py:71
  (143 shorter events, 156.0 us)
Async XLA Ops:
  6.5 91.5 %all-gather.45.cloned.1.call-start = ((), (), s32[]{:S(2)}) async-start(), calls=%async_computation.14 | async-start | bytes 9830400 | tf_op jit(solution)/shard_map/all_gather | solution.py:49
  12.9 190.7 %all-gather.33.cloned.1.call-start = ((), (), s32[]{:S(2)}) async-start(), calls=%async_computation.4 | async-start | bytes 23592960 | tf_op jit(solution)/shard_map/all_gather | solution.py:54
  16.6 230.9 %all-gather.43.cloned.1.call-start = ((), (), s32[]{:S(2)}) async-start(), calls=%async_computation.13 | async-start | bytes 1966080 | tf_op jit(solution)/shard_map/all_gather | solution.py:50
  20.0 251.2 %all-gather.41.cloned.1.call-start = ((), (), s32[]{:S(2)}) async-start(), calls=%async_computation.12 | async-start | bytes 1966080 | tf_op jit(solution)/shard_map/all_gather | solution.py:51
  22.5 311.6 %all-gather.47.cloned.1.call-start = ((), (), s32[]{:S(2)}) async-start(), calls=%async_computation.15 | async-start | bytes 9830400 | tf_op jit(solution)/shard_map/all_gather | solution.py:52
  28.7 570.8 %reduce-scatter.5.cloned.1.call-start = ((), (), s32[]{:S(2)}) async-start(), calls=%async_computation.5 | async-start | bytes 47185920 | tf_op jit(solution)/shard_map/reduce_scatter | solution.py:60
  28.8 242.3 %copy-start.11 = (pred[256,256]{0,1:T(8,128)(4,1)}, pred[256,256]{0,1:T(8,128)(4,1)S(1)}, u32[]{:S(2)}) copy-start(pred[256,256]{0,1:T(8,128)(4,1)S(1)} %iota_compare_fusion) | copy-start | bytes 196612
  28.9 230.9 %copy-start.13 = (f32[256,64]{1,0:T(8,128)}, f32[256,64]{1,0:T(8,128)S(1)}, u32[]{:S(2)}) copy-start(f32[256,64]{1,0:T(8,128)S(1)} %copy.28) | copy-start | bytes 196612
  29.0 230.8 %copy-start.15 = (f32[256,64]{1,0:T(8,128)}, f32[256,64]{1,0:T(8,128)S(1)}, u32[]{:S(2)}) copy-start(f32[256,64]{1,0:T(8,128)S(1)} %copy.30) | copy-start | bytes 196612
  247.5 12.2 copy-start.20
  247.5 12.4 copy-start.7
  247.5 12.4 copy-start.9
  360.9 450.0 %all-gather.49.cloned.1.call-start = ((), (), s32[]{:S(2)}) async-start(), calls=%async_computation.16 | async-start | bytes 26542080 | tf_op jit(solution)/shard_map/all_gather | solution.py:62
  372.9 543.6 %all-gather.35.cloned.1.call-start = ((), (), s32[]{:S(2)}) async-start(), calls=%async_computation.6 | async-start | bytes 23592960 | tf_op jit(solution)/shard_map/all_gather | solution.py:66
  606.8 521.2 %all-gather.51.cloned.1.call-start = ((), (), s32[]{:S(2)}) async-start(), calls=%async_computation.17 | async-start | bytes 26542080 | tf_op jit(solution)/shard_map/all_gather | solution.py:63
  618.7 720.6 %all-gather.53.cloned.1.call-start = ((), (), s32[]{:S(2)}) async-start(), calls=%async_computation.18 | async-start | bytes 26542080 | tf_op jit(solution)/shard_map/all_gather | solution.py:64
  630.7 998.3 %reduce-scatter.7.cloned.1.call-start = ((), (), s32[]{:S(2)}) async-start(), calls=%async_computation.7 | async-start | bytes 47185920 | tf_op jit(solution)/shard_map/reduce_scatter | solution.py:71
  1390.4 322.1 %all-gather.59.cloned.1.call-start = ((), (), s32[]{:S(2)}) async-start(), calls=%async_computation.21 | async-start | bytes 9830400 | tf_op jit(solution)/shard_map/all_gather | solution.py:49
  1391.0 242.4 %copy-start.23 = (f32[1,5120]{1,0:T(1,128)S(1)}, f32[1,5120]{1,0:T(1,128)}, u32[]{:S(2)}) copy-start(f32[1,5120]{1,0:T(1,128)} %get-tuple-element.39) | copy-start | bytes 61444
  1391.0 427.1 %all-gather.37.cloned.1.call-start = ((), (), s32[]{:S(2)}) async-start(), calls=%async_computation.8 | async-start | bytes 23592960 | tf_op jit(solution)/shard_map/all_gather | solution.py:54
  1635.7 226.5 %all-gather.57.cloned.1.call-start = ((), (), s32[]{:S(2)}) async-start(), calls=%async_computation.20 | async-start | bytes 1966080 | tf_op jit(solution)/shard_map/all_gather | solution.py:50
  1636.8 248.7 %all-gather.55.cloned.1.call-start = ((), (), s32[]{:S(2)}) async-start(), calls=%async_computation.19 | async-start | bytes 1966080 | tf_op jit(solution)/shard_map/all_gather | solution.py:51
  1637.4 311.1 %all-gather.61.cloned.1.call-start = ((), (), s32[]{:S(2)}) async-start(), calls=%async_computation.22 | async-start | bytes 9830400 | tf_op jit(solution)/shard_map/all_gather | solution.py:52
  1638.0 575.9 %reduce-scatter.9.cloned.1.call-start = ((), (), s32[]{:S(2)}) async-start(), calls=%async_computation.9 | async-start | bytes 47185920 | tf_op jit(solution)/shard_map/reduce_scatter | solution.py:60
  1862.1 12.1 copy-start.16
  1975.4 449.9 %all-gather.63.cloned.1.call-start = ((), (), s32[]{:S(2)}) async-start(), calls=%async_computation.23 | async-start | bytes 26542080 | tf_op jit(solution)/shard_map/all_gather | solution.py:62
  1976.0 243.0 %copy-start.22 = (f32[1,5120]{1,0:T(1,128)S(1)}, f32[1,5120]{1,0:T(1,128)}, u32[]{:S(2)}) copy-start(f32[1,5120]{1,0:T(1,128)} %get-tuple-element.37) | copy-start | bytes 61444
  1976.0 554.8 %all-gather.39.cloned.1.call-start = ((), (), s32[]{:S(2)}) async-start(), calls=%async_computation.10 | async-start | bytes 23592960 | tf_op jit(solution)/shard_map/all_gather | solution.py:66
  2221.2 520.9 %all-gather.65.cloned.1.call-start = ((), (), s32[]{:S(2)}) async-start(), calls=%async_computation.24 | async-start | bytes 26542080 | tf_op jit(solution)/shard_map/all_gather | solution.py:63
  2221.8 731.8 %all-gather.67.cloned.1.call-start = ((), (), s32[]{:S(2)}) async-start(), calls=%async_computation.25 | async-start | bytes 26542080 | tf_op jit(solution)/shard_map/all_gather | solution.py:64
  2222.6 1020.5 %reduce-scatter.11.cloned.1.call-start = ((), (), s32[]{:S(2)}) async-start(), calls=%async_computation.11 | async-start | bytes 47185920 | tf_op jit(solution)/shard_map/reduce_scatter | solution.py:71
  3004.5 238.6 %copy-start.3 = (bf16[8,32,5120]{2,1,0:T(8,128)(2,1)S(1)}, bf16[8,32,5120]{2,1,0:T(8,128)(2,1)}, u32[]{:S(2)}) copy-start(bf16[8,32,5120]{2,1,0:T(8,128)(2,1)} %copy-done.2) | copy-start | bytes 7864324
  (16 other events, 95.5 us)
Sparse Core Ops, SparseCore 0:
  13.0 84.9 all-gather.44
  99.9 103.6 all-gather.32
  205.1 22.0 all-gather.42
  228.5 22.0 all-gather.40
  252.0 82.1 all-gather.46
  361.1 238.3 reduce-scatter.4
  601.0 209.8 all-gather.48
  812.8 103.6 all-gather.34
  918.0 209.8 all-gather.50
  1129.4 209.8 all-gather.52
  1390.6 238.3 reduce-scatter.6
  1630.4 82.1 all-gather.58
  1714.4 103.6 all-gather.36
  1819.5 22.0 all-gather.56
  1842.9 22.0 all-gather.54
  1866.3 82.1 all-gather.60
  1975.5 238.3 reduce-scatter.8
  2215.3 209.8 all-gather.62
  2427.1 103.6 all-gather.38
  2532.2 209.8 all-gather.64
  2743.7 209.8 all-gather.66
  3004.6 238.3 reduce-scatter.10
where the time goes:
time: 3260 us; the launch traced here: 3250 us
  waiting for transfers between devices  2630 us (81%)
  matrix products  463 us (14%)
  local copies, waits for them, and re-layouts  111 us (3%)
  other arithmetic  34 us (1%)
    reduce_scatter x2, waiting for transfers between devices, device_step(): lax.psum_scatter(mlp_part, 'model', scatter_dimension=1, tiled=True)  476 us
    reduce_scatter x2, waiting for transfers between devices, device_step(): lax.psum_scatter(attn_part, 'model', scatter_dimension=1, tiled=True)  463 us
    all_gather x2, waiting for transfers between devices, device_step(): wg_full = lax.all_gather(w_gate[layer_idx], 'fsdp', axis=0, tiled=True)  383 us
    all_gather x2, waiting for transfers between devices, device_step(): wd_full = lax.all_gather(w_down[layer_idx], 'fsdp', axis=1, tiled=True)  331 us
    all_gather x2, waiting for transfers between devices, device_step(): wu_full = lax.all_gather(w_up[layer_idx], 'fsdp', axis=0, tiled=True)  331 us
    all_gather x2, waiting for transfers between devices, device_step(): normed_all = lax.all_gather(normed, 'model', axis=1, tiled=True)  211 us
    all_gather x2, waiting for transfers between devices, device_step(): mlp_in = lax.all_gather(normed_mlp, 'model', axis=1, tiled=True)  211 us
    all_gather x2, waiting for transfers between devices, device_step(): wq_full = lax.all_gather(w_q[layer_idx], 'fsdp', axis=0, tiled=True)  143 us
  transfers between devices with their start and end apart: 22, of which 18 were waited for; matrix products, arithmetic and copies ran while one was open for 13% of the time, Pallas kernels for 0%

commit v1 on v0

v1 whole, which is shorter than its diff:
```python
import functools

import jax
import jax.numpy as jnp
from jax import lax
from jax.experimental import pallas as pl
from jax.experimental.pallas import tpu as pltpu
from jax.sharding import PartitionSpec as P

EPS = 1e-5
MESH = pl.DeviceIdType.MESH
NT = (((1,), (1,)), ((), ()))
LD = 1
LX = 2
LT = LD + 2 * LX
LH = 2
F32 = jnp.float32
BF16 = jnp.bfloat16


def _norm(rows, gain):
    rows = rows.astype(F32)
    mean_sq = jnp.mean(rows * rows, axis=-1, keepdims=True)
    return (rows * lax.rsqrt(mean_sq + EPS) * gain).astype(BF16)


def _kernel(
    x_ref, ga_ref, gm_ref, cos_ref, sin_ref, wq_ref, wk_ref, wv_ref, wo_ref, wg_ref, wu_ref, wd_ref,
    y_ref, rq, rk, rv, ro, rg, ru, ha, hb,
    xbuf, mpeer, hst, hv, pown, psib, rd, t1, t2, rx, ry, rx2, ry2, hown, hrecv, cbuf, sbuf,
    zs, zr, gs, gr, ds, dr, xs, xr, ys, yr, x2s, x2r, y2s, y2r, ms, mr, os_, or_, hs, hr,
    sa, ra, sb, rb, loc, hvs, wl,
):
    n_layers = wq_ref.shape[0]
    NB, T, D = x_ref.shape
    W, V = D // 2, D // 4
    QW = wq_ref.shape[2]
    HD = wk_ref.shape[2]
    HB = wg_ref.shape[1] // 2
    R = 8 * T
    NU = 2 * NB

    z = lax.axis_index("fsdp")
    m = lax.axis_index("model")
    y, x, c, q = m // 4, (m // 2) % 2, m % 2, m // 2
    qx, qy, qd = q + 1 - 2 * x, q + 2 - 4 * y, 3 - q
    zp, xp, yp, sp = (1 - z, m), (z, m + 2 - 4 * x), (z, m + 4 - 8 * y), (z, m + 1 - 2 * c)
    mine = pl.ds(pl.multiple_of(z * W, 128), W)
    other = pl.ds(pl.multiple_of((1 - z) * W, 128), W)

    barrier = pltpu.get_barrier_semaphore()
    for dev in (zp, xp, yp, sp):
        pl.semaphore_signal(barrier, inc=1, device_id=dev, device_id_type=MESH)
    pl.semaphore_wait(barrier, 4)

    def send(src, dst, s, r, dev):
        return pltpu.make_async_remote_copy(
            src_ref=src, dst_ref=dst, send_sem=s, recv_sem=r, device_id=dev, device_id_type=MESH)

    def z_q(l):
        return send(wq_ref.at[l], rq.at[l], zs.at[0], zr.at[0], zp)

    def z_k(l):
        return send(wk_ref.at[l], rk.at[l], zs.at[1], zr.at[1], zp)

    def z_v(l):
        return send(wv_ref.at[l], rv.at[l], zs.at[2], zr.at[2], zp)

    def z_o(l):
        return send(wo_ref.at[l], ro.at[l], zs.at[3], zr.at[3], zp)

    theirs_h = pl.ds(pl.multiple_of((1 - z) * HB, 16), HB)

    def z_g(l):
        return send(wg_ref.at[l, theirs_h], rg.at[l], gs.at[0], gr.at[0], zp)

    def z_u(l):
        return send(wu_ref.at[l, theirs_h], ru.at[l], gs.at[1], gr.at[1], zp)

    CR = HB // 9

    def z_gate_up_part(l, k):
        j = k % 9
        src = pl.ds(pl.multiple_of((1 - z) * HB + j * CR, 16), CR)
        dst = pl.ds(pl.multiple_of(j * CR, 16), CR)

        @pl.when(k < 9)
        def _():
            send(wg_ref.at[l, src], rg.at[l, dst], gs.at[0], gr.at[0], zp).start()

        @pl.when(k >= 9)
        def _():
            send(wu_ref.at[l, src], ru.at[l, dst], gs.at[1], gr.at[1], zp).start()

    QR, OR = W // 8, QW // 8

    def z_attn_part(l, k):
        i = k // 2

        @pl.when(k % 2 == 0)
        def _():
            rows = pl.ds(pl.multiple_of(i * QR, 16), QR)
            send(wq_ref.at[l, rows], rq.at[l, rows], zs.at[0], zr.at[0], zp).start()
            send(wk_ref.at[l, rows], rk.at[l, rows], zs.at[1], zr.at[1], zp).start()
            send(wv_ref.at[l, rows], rv.at[l, rows], zs.at[2], zr.at[2], zp).start()

        @pl.when(k % 2 == 1)
        def _():
            rows = pl.ds(pl.multiple_of(i * OR, 16), OR)
            send(wo_ref.at[l, rows], ro.at[l, rows], zs.at[3], zr.at[3], zp).start()

    lo, hi = pl.ds(0, W), pl.ds(W, W)

    def ag_own(h, s, r, u):
        return (send(h.at[u, 0, q], h.at[u, 0, q], s.at[u, 0], r.at[u, 0], xp),
                send(h.at[u, 0, q], h.at[u, 0, q], s.at[u, 1], r.at[u, 1], yp))

    def ag_fwd(h, s, r, u):
        return (send(h.at[u, 0, qx, :, lo], h.at[u, 0, qx, :, lo], s.at[u, 2], r.at[u, 2], yp),
                send(h.at[u, 0, qy, :, hi], h.at[u, 0, qy, :, hi], s.at[u, 3], r.at[u, 3], xp))

    def ag_sib(h, s, r, u):
        return send(h.at[u, 0], h.at[u, 1], s.at[u, 4], r.at[u, 4], sp)

    def ag_send_own(h, s, r, u):
        for d in ag_own(h, s, r, u):
            d.start()

    def ag_fwd1(h, s, r, u):
        own_x, own_y = ag_own(h, s, r, u)
        fwd_y, fwd_x = ag_fwd(h, s, r, u)
        own_x.wait_recv()
        fwd_y.start()
        own_y.wait_recv()
        fwd_x.start()

    def ag_fwd2(h, s, r, u):
        fwd_y, fwd_x = ag_fwd(h, s, r, u)
        fwd_y.wait_recv()
        fwd_x.wait_recv()
        ag_sib(h, s, r, u).start()

    def ag_local(h, u):
        return pltpu.make_async_copy(h.at[u], hv.at[u % 2], hvs.at[u % 2])

    def ag_load(h, s, r, u):
        ag_sib(h, s, r, u).wait_recv()
        ag_local(h, u).start()

    def ag_finish(h, s, r, u):
        ag_local(h, u).wait()
        for d in ag_own(h, s, r, u) + ag_fwd(h, s, r, u) + (ag_sib(h, s, r, u),):
            d.wait_send()

    def h_store(h, u, i, j):
        return pltpu.make_async_copy(hst.at[i, j], h.at[u, 0, q], loc.at[i, j])

    def rs_d(u):
        return send(psib.at[u % 2], rd.at[u % 2], ds.at[u % 2], dr.at[u % 2], sp)

    def rs_x(u):
        i = u % 4
        return send(pown.at[i, :, 1 - x, :, pl.ds(0, V)], rx.at[i], xs.at[i], xr.at[i], xp)

    def rs_y(u):
        i = u % 4
        return send(pown.at[i, 1 - y, :, :, pl.ds(V, V)], ry.at[i], ys.at[i], yr.at[i], yp)

    def rs_x2(u):
        i = u % 4
        return send(t2.at[i, 1 - x], rx2.at[i], x2s.at[i], x2r.at[i], xp)

    def rs_y2(u):
        i = u % 4
        return send(t1.at[i, 1 - y], ry2.at[i], y2s.at[i], y2r.at[i], yp)

    def store_product(u, pairs):
        half = W // 2
        for j in range(2):
            cols = pl.ds(j * half, half)
            acc = None
            for a, w, rows in pairs:
                wv_ = w[:, cols] if rows is None else w[rows, cols]
                p = jnp.dot(a, wv_, preferred_element_type=F32)
                acc = p if acc is None else acc + p
            pown[u % 4, :, :, :, cols] = acc[: R // 2].reshape(2, 2, T, half)
            psib[u % 2, :, :, :, cols] = acc[R // 2:].reshape(2, 2, T, half)

    def rs_stage2(u):
        rs_d(u).wait()
        pown[u % 4] = pown[u % 4] + rd[u % 2]

    def rs_stage3(u):
        i = u % 4
        rs_x(u).wait()
        rs_y(u).wait()
        t1[i] = pown[i, :, x, :, pl.ds(0, V)] + rx[i]
        t2[i] = pown[i, y, :, :, pl.ds(V, V)] + ry[i]

    def rs_stage4(u):
        i = u % 4
        rs_x2(u).wait()
        rs_y2(u).wait()
        return t1[i, y] + ry2[i], t2[i, x] + rx2[i]

    def rs_steps(k, n, finish):
        @pl.when(jnp.logical_and(k >= LD, k < n + LD))
        def _():
            rs_stage2(k - LD)

        @pl.when(jnp.logical_and(k >= LD + LX, k < n + LD + LX))
        def _():
            rs_stage3(k - LD - LX)

        @pl.when(jnp.logical_and(k >= LT, k < n + LT))
        def _():
            finish(k - LT, *rs_stage4(k - LT))

    def rs_sends(k, n):
        @pl.when(jnp.logical_and(k >= 0, k < n))
        def _():
            rs_d(k).start()

        @pl.when(jnp.logical_and(k >= LD, k < n + LD))
        def _():
            rs_x(k - LD).start()
            rs_y(k - LD).start()

        @pl.when(jnp.logical_and(k >= LD + LX, k < n + LD + LX))
        def _():
            rs_x2(k - LD - LX).start()
            rs_y2(k - LD - LX).start()

    def m_send(b):
        return send(xbuf.at[b], mpeer.at[b], ms.at[b], mr.at[b], zp)

    def out_send(b):
        return send(mpeer.at[b, :, mine], xbuf.at[b, :, mine], os_.at[b], or_.at[b], zp)

    def hid_send(u):
        i = u % 4
        return send(hown.at[i], hrecv.at[i], hs.at[i], hr.at[i], zp)

    for d in (z_q(0), z_k(0), z_v(0), z_o(0)):
        d.start()
    first = [pltpu.make_async_copy(x_ref, xbuf, wl.at[0]),
             pltpu.make_async_copy(cos_ref.at[:, c], cbuf.at[0], wl.at[1]),
             pltpu.make_async_copy(cos_ref.at[:, 1 - c], cbuf.at[1], wl.at[2]),
             pltpu.make_async_copy(sin_ref.at[:, c], sbuf.at[0], wl.at[3]),
             pltpu.make_async_copy(sin_ref.at[:, 1 - c], sbuf.at[1], wl.at[4])]
    for d in first:
        d.start()
    for d in first:
        d.wait()

    def first_rows(b, carry):
        hst[b % 2, 0] = _norm(xbuf[b], ga_ref[0])
        d = h_store(ha.at[0], b, b % 2, 0)
        d.start()
        d.wait()
        ag_send_own(ha.at[0], sa, ra, b)
        return carry

    lax.fori_loop(0, NB, first_rows, 0)

    def pos_of(r):
        return 2 * T * ((r // T) % 4) + T * ((c + r // (4 * T)) % 2) + r % T

    def loop_a(l, wa_o, wa_r, wo_o, wo_r, o_all):
        h = ha.at[l]
        hbl = hb.at[l]
        loads = [pltpu.make_async_copy(wq_ref.at[l], wa_o.at[:, pl.ds(0, QW)], wl.at[0]),
                 pltpu.make_async_copy(wk_ref.at[l], wa_o.at[:, pl.ds(QW, HD)], wl.at[1]),
                 pltpu.make_async_copy(wv_ref.at[l], wa_o.at[:, pl.ds(QW + HD, HD)], wl.at[2]),
                 pltpu.make_async_copy(wo_ref.at[l], wo_o, wl.at[3])]
        for d in loads:
            d.start()
        ag_fwd1(h, sa, ra, 0)
        ag_fwd1(h, sa, ra, 1)
        ag_fwd2(h, sa, ra, 0)
        ag_load(h, sa, ra, 0)
        for d in (z_q(l), z_k(l), z_v(l)):
            d.wait()
        more = [pltpu.make_async_copy(rq.at[l], wa_r.at[:, pl.ds(0, QW)], wl.at[4]),
                pltpu.make_async_copy(rk.at[l], wa_r.at[:, pl.ds(QW, HD)], wl.at[5]),
                pltpu.make_async_copy(rv.at[l], wa_r.at[:, pl.ds(QW + HD, HD)], wl.at[6])]
        for d in more:
            d.start()
        for d in loads + more:
            d.wait()

        def finish(u, low, high):
            b = u % NB
            off = (z + (u // NB) * (1 - 2 * z)) * W
            ca = pl.ds(pl.multiple_of(off, 128), V)
            cb = pl.ds(pl.multiple_of(off + V, 128), V)
            xbuf[b, :, ca] = (xbuf[b, :, ca].astype(F32) + low).astype(BF16)
            xbuf[b, :, cb] = (xbuf[b, :, cb].astype(F32) + high).astype(BF16)

        def step(k, carry):
            @pl.when(k + 2 < NB)
            def _():
                ag_fwd1(h, sa, ra, k + 2)

            @pl.when(k + 1 < NB)
            def _():
                ag_fwd2(h, sa, ra, k + 1)

            @pl.when(k < NB)
            def _():
                ag_finish(h, sa, ra, k)
                i = k % 2
                acc = jnp.dot(hv[i, :, :, :, mine].reshape(R, W), wa_o[...], preferred_element_type=F32)
                acc += jnp.dot(hv[i, :, :, :, other].reshape(R, W), wa_r[...], preferred_element_type=F32)
                qkv = acc.astype(BF16)
                cosv = cbuf[...].reshape(R, HD)
                sinv = sbuf[...].reshape(R, HD)

                def rope(t):
                    t = t.astype(F32)
                    return (t * cosv + pltpu.roll(t, HD // 2, 1) * sinv).astype(BF16)

                mask = pos_of(lax.broadcasted_iota(jnp.int32, (R, R), 0)) >= pos_of(
                    lax.broadcasted_iota(jnp.int32, (R, R), 1))
                kk = rope(qkv[:, QW:QW + HD])
                vv = qkv[:, QW + HD:]
                for g in range(QW // HD):
                    s = lax.dot_general(rope(qkv[:, g * HD:(g + 1) * HD]), kk, NT, preferred_element_type=F32)
                    s = jnp.where(mask, s * HD ** -0.5, -jnp.inf)
                    e = jnp.exp(s - jnp.max(s, axis=-1, keepdims=True))
                    p = (e / jnp.sum(e, axis=-1, keepdims=True)).astype(BF16)
                    o_all[k, :, g * HD:(g + 1) * HD] = jnp.dot(p, vv, preferred_element_type=F32).astype(BF16)
                store_product(k, [(o_all[k], wo_o, None)])

            @pl.when(k == NB)
            def _():
                z_o(l).wait()
                d = pltpu.make_async_copy(ro.at[l], wo_r, wl.at[7])
                d.start()
                d.wait()

            @pl.when(jnp.logical_and(k >= NB, k < NU))
            def _():
                store_product(k, [(o_all[k - NB], wo_r, None)])

            rs_steps(k, NU, finish)

            @pl.when(k + 1 < NB)
            def _():
                ag_load(h, sa, ra, k + 1)

            rs_sends(k, NU)

            k0 = NB + LT

            @pl.when(jnp.logical_and(k >= k0, k < k0 + NB))
            def _():
                b = k - k0
                hst[b % 2, 0] = _norm(xbuf[b], gm_ref[l])
                h_store(hbl, 2 * b + z, b % 2, 0).start()
                m_send(b).start()

            @pl.when(jnp.logical_and(k >= k0 + 1, k < k0 + 1 + NB))
            def _():
                b = k - k0 - 1
                h_store(hbl, 2 * b + z, b % 2, 0).wait()
                ag_send_own(hbl, sb, rb, 2 * b + z)
                m_send(b).wait()
                hst[b % 2, 1] = _norm(mpeer[b], gm_ref[l])
                h_store(hbl, 2 * b + 1 - z, b % 2, 1).start()

            @pl.when(jnp.logical_and(k >= k0 + 2, k < k0 + 2 + NB))
            def _():
                b = k - k0 - 2
                h_store(hbl, 2 * b + 1 - z, b % 2, 1).wait()
                ag_send_own(hbl, sb, rb, 2 * b + 1 - z)

            @pl.when(k < 18)
            def _():
                z_gate_up_part(l, k)

            return carry

        lax.fori_loop(0, NU + LT + 2, step, 0)

    def loop_b(l, g_o, g_r, u_o, u_r, wd_v):
        h = hb.at[l]
        mine_h = pl.ds(pl.multiple_of(z * HB, 16), HB)
        loads = [pltpu.make_async_copy(wg_ref.at[l, mine_h], g_o, wl.at[0]),
                 pltpu.make_async_copy(wu_ref.at[l, mine_h], u_o, wl.at[1]),
                 pltpu.make_async_copy(wd_ref.at[l], wd_v, wl.at[2])]
        for d in loads:
            d.start()
        ag_fwd1(h, sb, rb, 0)
        ag_fwd1(h, sb, rb, 1)
        ag_fwd2(h, sb, rb, 0)
        ag_load(h, sb, rb, 0)
        for d in (z_g(l), z_u(l)):
            d.wait()
        more = [pltpu.make_async_copy(rg.at[l], g_r, wl.at[3]),
                pltpu.make_async_copy(ru.at[l], u_r, wl.at[4])]
        for d in more:
            d.start()
        for d in loads + more:
            d.wait()

        def finish(s, low, high):
            b = s // 2
            ca = pl.ds(pl.multiple_of(z * W, 128), V)
            cb = pl.ds(pl.multiple_of(z * W + V, 128), V)

            @pl.when(s % 2 == z)
            def _():
                xbuf[b, :, ca] = (xbuf[b, :, ca].astype(F32) + low).astype(BF16)
                xbuf[b, :, cb] = (xbuf[b, :, cb].astype(F32) + high).astype(BF16)

            @pl.when(s % 2 == 1 - z)
            def _():
                mpeer[b, :, ca] = (mpeer[b, :, ca].astype(F32) + low).astype(BF16)
                mpeer[b, :, cb] = (mpeer[b, :, cb].astype(F32) + high).astype(BF16)

        def step(k, carry):
            @pl.when(k + 2 < NU)
            def _():
                ag_fwd1(h, sb, rb, k + 2)

            @pl.when(k + 1 < NU)
            def _():
                ag_fwd2(h, sb, rb, k + 1)

            @pl.when(k < NU)
            def _():
                ag_finish(h, sb, rb, k)
                i = k % 2
                hm = hv[i, :, :, :, mine].reshape(R, W)
                ho = hv[i, :, :, :, other].reshape(R, W)
                gate = lax.dot_general(hm, g_o[...], NT, preferred_element_type=F32)
                gate += lax.dot_general(ho, g_r[...], NT, preferred_element_type=F32)
                up = lax.dot_general(hm, u_o[...], NT, preferred_element_type=F32)
                up += lax.dot_general(ho, u_r[...], NT, preferred_element_type=F32)
                hown[k % 4] = (jax.nn.silu(gate) * up).astype(BF16)

            v = k - LH

            @pl.when(jnp.logical_and(v >= 0, v < NU))
            def _():
                hid_send(v).wait()
                store_product(v, [(hown[v % 4], wd_v, mine_h), (hrecv[v % 4], wd_v, theirs_h)])

            rs_steps(v, NU, finish)

            @pl.when(k + 1 < NU)
            def _():
                ag_load(h, sb, rb, k + 1)

            @pl.when(k < NU)
            def _():
                hid_send(k).start()

            rs_sends(v, NU)

            s = v - LT

            @pl.when(jnp.logical_and(jnp.logical_and(s >= 0, s < NU), s % 2 == 1 - z))
            def _():
                out_send(s // 2).start()

            @pl.when(jnp.logical_and(jnp.logical_and(s >= 2, s < NU + 2), s % 2 == 0))
            def _():
                b = s // 2 - 1
                out_send(b).wait()

                @pl.when(l + 1 < n_layers)
                def _():
                    hst[b % 2, 0] = _norm(xbuf[b], ga_ref[(l + 1) % n_layers])
                    h_store(ha.at[(l + 1) % n_layers], b, b % 2, 0).start()

            @pl.when(jnp.logical_and(l + 1 < n_layers, jnp.logical_and(jnp.logical_and(s >= 3, s < NU + 3), s % 2 == 1)))
            def _():
                b = s // 2 - 1
                h_store(ha.at[(l + 1) % n_layers], b, b % 2, 0).wait()
                ag_send_own(ha.at[(l + 1) % n_layers], sa, ra, b)

            @pl.when(jnp.logical_and(l + 1 < n_layers, k < 16))
            def _():
                z_attn_part((l + 1) % n_layers, k)

            return carry

        lax.fori_loop(0, NU + LH + LT + 2, step, 0)

    def layer(l, carry):
        pl.run_scoped(
            functools.partial(loop_a, l),
            pltpu.VMEM((W, QW + 2 * HD), BF16), pltpu.VMEM((W, QW + 2 * HD), BF16),
            pltpu.VMEM((QW, W), BF16), pltpu.VMEM((QW, W), BF16), pltpu.VMEM((NB, R, QW), BF16))
        pl.run_scoped(
            functools.partial(loop_b, l),
            pltpu.VMEM((HB, W), BF16), pltpu.VMEM((HB, W), BF16),
            pltpu.VMEM((HB, W), BF16), pltpu.VMEM((HB, W), BF16), pltpu.VMEM((2 * HB, W), BF16))
        return carry

    lax.fori_loop(0, n_layers, layer, 0)
    d = pltpu.make_async_copy(xbuf, y_ref, wl.at[0])
    d.start()
    d.wait()


def solution(mesh):
    act_spec = P("fsdp", "model", None)
    col_spec = P(None, "fsdp", "model")
    row_spec = P(None, "model", "fsdp")

    def device_step(x_in, gain_attn, gain_mlp, rope_cos, rope_sin, w_q, w_k, w_v, w_o, w_gate, w_up, w_down):
        L = w_q.shape[0]
        NB, T, D = x_in.shape
        W, V = D // 2, D // 4
        HB = w_gate.shape[2] // 2
        NU, R = 2 * NB, 8 * T
        half = rope_cos.shape[1]
        cos2 = jnp.concatenate([rope_cos, rope_cos], axis=1).reshape(4, 2, T, 2 * half)
        sin2 = jnp.concatenate([-rope_sin, rope_sin], axis=1).reshape(4, 2, T, 2 * half)
        hbm = pl.BlockSpec(memory_space=pl.ANY)
        vmem = pl.BlockSpec(memory_space=pltpu.VMEM)
        dma = pltpu.SemaphoreType.DMA
        sds = jax.ShapeDtypeStruct
        outs = pl.pallas_call(
            _kernel,
            name="two_layers",
            in_specs=[hbm, vmem, vmem] + [hbm] * 9,
            out_specs=[hbm] * 9,
            out_shape=[
                sds(x_in.shape, BF16), sds(w_q.shape, BF16), sds(w_k.shape, BF16), sds(w_v.shape, BF16),
                sds(w_o.shape, BF16), sds((L, HB, W), BF16), sds((L, HB, W), BF16),
                sds((L, NB, 2, 4, T, D), BF16), sds((L, NU, 2, 4, T, D), BF16)],
            scratch_shapes=[
                pltpu.VMEM((NB, T, D), BF16), pltpu.VMEM((NB, T, D), BF16), pltpu.VMEM((2, 2, T, D), BF16),
                pltpu.VMEM((2, 2, 4, T, D), BF16),
                pltpu.VMEM((4, 2, 2, T, W), F32), pltpu.VMEM((2, 2, 2, T, W), F32), pltpu.VMEM((2, 2, 2, T, W), F32),
                pltpu.VMEM((4, 2, T, V), F32), pltpu.VMEM((4, 2, T, V), F32),
                pltpu.VMEM((4, 2, T, V), F32), pltpu.VMEM((4, 2, T, V), F32),
                pltpu.VMEM((4, T, V), F32), pltpu.VMEM((4, T, V), F32),
                pltpu.VMEM((4, R, HB), BF16), pltpu.VMEM((4, R, HB), BF16),
                pltpu.VMEM((2, 4, T, 2 * half), F32), pltpu.VMEM((2, 4, T, 2 * half), F32),
                dma((4,)), dma((4,)), dma((2,)), dma((2,)), dma((2,)), dma((2,)),
                dma((4,)), dma((4,)), dma((4,)), dma((4,)), dma((4,)), dma((4,)), dma((4,)), dma((4,)),
                dma((NB,)), dma((NB,)), dma((NB,)), dma((NB,)), dma((4,)), dma((4,)),
                dma((NB, 5)), dma((NB, 5)), dma((NU, 5)), dma((NU, 5)), dma((2, 2)), dma((2,)), dma((8,))],
            compiler_params=pltpu.CompilerParams(
                collective_id=0, has_side_effects=True, vmem_limit_bytes=67_000_000),
        )(x_in, gain_attn[:, None], gain_mlp[:, None], cos2, sin2, w_q, w_k, w_v, w_o,
          jnp.swapaxes(w_gate, 1, 2), jnp.swapaxes(w_up, 1, 2), w_down)
        return outs[0]

    return jax.shard_map(
        device_step, mesh=mesh,
        in_specs=(act_spec, P(), P(), P(), P(), col_spec, col_spec, col_spec, row_spec, col_spec, col_spec, row_spec),
        out_specs=act_spec, check_vma=False)
```

time: 3260 us -> 1450 us (0.44)
  waiting for transfers between devices: 2630 us -> 0 us
  Pallas kernels: 0 us -> 1440 us
  matrix products: 463 us -> 0 us
  local copies, waits for them, and re-layouts: 111 us -> 7.75 us
    all_gather x18 -> x0, waiting for transfers between devices: 1690 us -> none  [the longest x2 383 us: device_step(): wg_full = lax.all_gather(w_gate[layer_idx], 'fsdp', axis=0, tiled=True)]
    pallas_call x0 -> x1, Pallas kernels: none -> 1440 us  [device_step(): pl.pallas_call(_kernel, name='two_layers', in_specs=[hbm, vmem, vmem] + [...]
    reduce_scatter x4 -> x0, waiting for transfers between devices: 940 us -> none  [the longest x2 476 us: device_step(): lax.psum_scatter(mlp_part, 'model', scatter_dimension=1, tiled=True)]
    dot_general x16 -> x0, matrix products: 463 us -> none  [the longest x2 102 us: device_step(): jnp.einsum('bsf,fd->bsd', hidden, wd_full, preferred_element_type=jnp.flo...]
    slice x11 -> x0, local copies, waits for them, and re-layouts: 65.1 us -> none  [the longest x1 12 us: device_step(): wd_full = lax.all_gather(w_down[layer_idx], 'fsdp', axis=1, tiled=True)]
  transfers between devices with their start and end apart: 22 -> 0, of which waited for: 18 -> 0; matrix products, arithmetic and copies ran while one was open for 13% -> 0% of each run, Pallas kernels for 0% -> 0%
where the time goes in v1:
time: 1450 us
  Pallas kernels  1440 us (99%)
    pallas_call x1, Pallas kernels, device_step(): pl.pallas_call(_kernel, name='two_layers', in_specs=[hbm, vmem, vmem] + [...  1440 us

profile of v1, /device:TPU:0, one launch (start us, length us, event | category | flops | bytes accessed | tf_op | source)
XLA Modules:
  0.0 1446.8 jit_solution(9579352088640625351)
XLA Ops:
  0.0 1.4 broadcast_in_dim.6.ga_ref
  1.4 1.4 broadcast_in_dim.7.gm_ref
  2.8 0.8 neg.3
  3.7 0.8 pad_maximum_fusion.1
  4.5 0.8 copy.14
  5.3 0.9 pad_maximum_fusion
  6.2 0.8 copy.13
  7.0 1436.4 %two_layers.1 = (bf16[8,32,5120]{2,1,0:T(8,128)(2,1)}, bf16[2,2560,640]{2,1,0:T(8,128)(2,1)}, bf16[2,2560,128]{2,1,0:T(8,128)(2,1)}, bf16[2,2560,128]{2,1,0:T(8,...) custom-call(bf16[8,32,5120]{2,1,0:T(8,128)(2,1)} %x_ref.1, ...), custom_call_target="tpu_custom_call" | custom-call | tf_op jit(solution)/shard_map/two_layers/pallas_call | solution.py:527
  1443.4 3.4 copy.16

commit v2 on v1

v2 whole, which is shorter than its diff:
```python
import functools

import jax
import jax.numpy as jnp
from jax import lax
from jax.experimental import pallas as pl
from jax.experimental.pallas import tpu as pltpu
from jax.sharding import PartitionSpec as P

EPS = 1e-5
MESH = pl.DeviceIdType.MESH
NT = (((1,), (1,)), ((), ()))
LD = 1
LX = 2
LT = LD + 2 * LX
LH = 2
F32 = jnp.float32
BF16 = jnp.bfloat16


def _norm(rows, gain):
    rows = rows.astype(F32)
    mean_sq = jnp.mean(rows * rows, axis=-1, keepdims=True)
    return (rows * lax.rsqrt(mean_sq + EPS) * gain).astype(BF16)


def _kernel(
    x_ref, ga_ref, gm_ref, cos_ref, sin_ref, wq_ref, wk_ref, wv_ref, wo_ref, wg_ref, wu_ref, wd_ref,
    y_ref, rq, rk, rv, ro, rg, ru, ha, hb,
    xbuf, mpeer, hst, hv, pown, psib, rd, t1, t2, rx, ry, rx2, ry2, hown, hrecv, cbuf, sbuf, tmp,
    zs, zr, gs, gr, ds, dr, xs, xr, ys, yr, x2s, x2r, y2s, y2r, ms, mr, os_, or_, hs, hr,
    sa, ra, sb, rb, loc, hvs, wl,
):
    n_layers = wq_ref.shape[0]
    NB, T, D = x_ref.shape
    W, V = D // 2, D // 4
    QW = wq_ref.shape[2]
    HD = wk_ref.shape[2]
    HB = wg_ref.shape[1] // 2
    R = 8 * T
    NU = 2 * NB

    z = lax.axis_index("fsdp")
    m = lax.axis_index("model")
    y, x, c, q = m // 4, (m // 2) % 2, m % 2, m // 2
    qx, qy, qd = q + 1 - 2 * x, q + 2 - 4 * y, 3 - q
    zp, xp, yp, sp = (1 - z, m), (z, m + 2 - 4 * x), (z, m + 4 - 8 * y), (z, m + 1 - 2 * c)
    mine = pl.ds(pl.multiple_of(z * W, 128), W)
    other = pl.ds(pl.multiple_of((1 - z) * W, 128), W)

    barrier = pltpu.get_barrier_semaphore()
    for dev in (zp, xp, yp, sp):
        pl.semaphore_signal(barrier, inc=1, device_id=dev, device_id_type=MESH)
    pl.semaphore_wait(barrier, 4)

    def send(src, dst, s, r, dev):
        return pltpu.make_async_remote_copy(
            src_ref=src, dst_ref=dst, send_sem=s, recv_sem=r, device_id=dev, device_id_type=MESH)

    def z_q(l):
        return send(wq_ref.at[l], rq.at[l], zs.at[0], zr.at[0], zp)

    def z_k(l):
        return send(wk_ref.at[l], rk.at[l], zs.at[1], zr.at[1], zp)

    def z_v(l):
        return send(wv_ref.at[l], rv.at[l], zs.at[2], zr.at[2], zp)

    def z_o(l):
        return send(wo_ref.at[l], ro.at[l], zs.at[3], zr.at[3], zp)

    theirs_h = pl.ds(pl.multiple_of((1 - z) * HB, 16), HB)

    def z_g(l):
        return send(wg_ref.at[l, theirs_h], rg.at[l], gs.at[0], gr.at[0], zp)

    def z_u(l):
        return send(wu_ref.at[l, theirs_h], ru.at[l], gs.at[1], gr.at[1], zp)

    CR = HB // 9

    def z_gate_up_part(l, k):
        j = k % 9
        src = pl.ds(pl.multiple_of((1 - z) * HB + j * CR, 16), CR)
        dst = pl.ds(pl.multiple_of(j * CR, 16), CR)

        @pl.when(k < 9)
        def _():
            send(wg_ref.at[l, src], rg.at[l, dst], gs.at[0], gr.at[0], zp).start()

        @pl.when(k >= 9)
        def _():
            send(wu_ref.at[l, src], ru.at[l, dst], gs.at[1], gr.at[1], zp).start()

    QR, OR = W // 8, QW // 8

    def z_qkv_part(l, i):
        rows = pl.ds(pl.multiple_of(i * QR, 16), QR)
        send(wq_ref.at[l, rows], rq.at[l, rows], zs.at[0], zr.at[0], zp).start()
        send(wk_ref.at[l, rows], rk.at[l, rows], zs.at[1], zr.at[1], zp).start()
        send(wv_ref.at[l, rows], rv.at[l, rows], zs.at[2], zr.at[2], zp).start()

    def z_o_part(l, i):
        rows = pl.ds(pl.multiple_of(i * OR, 16), OR)
        send(wo_ref.at[l, rows], ro.at[l, rows], zs.at[3], zr.at[3], zp).start()

    lo, hi = pl.ds(0, W), pl.ds(W, W)

    def ag_own(h, s, r, u):
        return (send(h.at[u, 0, q], h.at[u, 0, q], s.at[u, 0], r.at[u, 0], xp),
                send(h.at[u, 0, q], h.at[u, 0, q], s.at[u, 1], r.at[u, 1], yp))

    def ag_fwd(h, s, r, u):
        return (send(h.at[u, 0, qx, :, lo], h.at[u, 0, qx, :, lo], s.at[u, 2], r.at[u, 2], yp),
                send(h.at[u, 0, qy, :, hi], h.at[u, 0, qy, :, hi], s.at[u, 3], r.at[u, 3], xp))

    def ag_sib(h, s, r, u):
        return send(h.at[u, 0], h.at[u, 1], s.at[u, 4], r.at[u, 4], sp)

    def ag_send_own(h, s, r, u):
        for d in ag_own(h, s, r, u):
            d.start()

    def ag_fwd1(h, s, r, u):
        own_x, own_y = ag_own(h, s, r, u)
        fwd_y, fwd_x = ag_fwd(h, s, r, u)
        own_x.wait_recv()
        fwd_y.start()
        own_y.wait_recv()
        fwd_x.start()

    def ag_fwd2(h, s, r, u):
        fwd_y, fwd_x = ag_fwd(h, s, r, u)
        fwd_y.wait_recv()
        fwd_x.wait_recv()
        ag_sib(h, s, r, u).start()

    def ag_local(h, u):
        return pltpu.make_async_copy(h.at[u], hv.at[u % 2], hvs.at[u % 2])

    def ag_load(h, s, r, u):
        ag_sib(h, s, r, u).wait_recv()
        ag_local(h, u).start()

    def ag_finish(h, s, r, u):
        ag_local(h, u).wait()
        for d in ag_own(h, s, r, u) + ag_fwd(h, s, r, u) + (ag_sib(h, s, r, u),):
            d.wait_send()

    def h_store(h, u, i, j):
        return pltpu.make_async_copy(hst.at[i, j], h.at[u, 0, q], loc.at[i, j])

    def rs_d(u):
        return send(psib.at[u % 2], rd.at[u % 2], ds.at[u % 2], dr.at[u % 2], sp)

    def rs_x(u):
        i = u % 4
        return send(pown.at[i, :, 1 - x, :, pl.ds(0, V)], rx.at[i], xs.at[i], xr.at[i], xp)

    def rs_y(u):
        i = u % 4
        return send(pown.at[i, 1 - y, :, :, pl.ds(V, V)], ry.at[i], ys.at[i], yr.at[i], yp)

    def rs_x2(u):
        i = u % 4
        return send(t2.at[i, 1 - x], rx2.at[i], x2s.at[i], x2r.at[i], xp)

    def rs_y2(u):
        i = u % 4
        return send(t1.at[i, 1 - y], ry2.at[i], y2s.at[i], y2r.at[i], yp)

    def store_product(u, pairs):
        half = W // 2
        for j in range(2):
            cols = pl.ds(j * half, half)
            acc = None
            for a, w, rows in pairs:
                wv_ = w[:, cols] if rows is None else w[rows, cols]
                p = jnp.dot(a, wv_, preferred_element_type=F32)
                acc = p if acc is None else acc + p
            pown[u % 4, :, :, :, cols] = acc[: R // 2].reshape(2, 2, T, half)
            psib[u % 2, :, :, :, cols] = acc[R // 2:].reshape(2, 2, T, half)

    def rs_stage2(u):
        rs_d(u).wait()
        pown[u % 4] = pown[u % 4] + rd[u % 2]

    def rs_stage3(u):
        i = u % 4
        rs_x(u).wait()
        rs_y(u).wait()
        t1[i] = pown[i, :, x, :, pl.ds(0, V)] + rx[i]
        t2[i] = pown[i, y, :, :, pl.ds(V, V)] + ry[i]

    def rs_stage4(u):
        i = u % 4
        rs_x2(u).wait()
        rs_y2(u).wait()
        return t1[i, y] + ry2[i], t2[i, x] + rx2[i]

    def rs_steps(k, n, finish):
        @pl.when(jnp.logical_and(k >= LD, k < n + LD))
        def _():
            rs_stage2(k - LD)

        @pl.when(jnp.logical_and(k >= LD + LX, k < n + LD + LX))
        def _():
            rs_stage3(k - LD - LX)

        @pl.when(jnp.logical_and(k >= LT, k < n + LT))
        def _():
            finish(k - LT, *rs_stage4(k - LT))

    def rs_sends(k, n):
        @pl.when(jnp.logical_and(k >= 0, k < n))
        def _():
            rs_d(k).start()

        @pl.when(jnp.logical_and(k >= LD, k < n + LD))
        def _():
            rs_x(k - LD).start()
            rs_y(k - LD).start()

        @pl.when(jnp.logical_and(k >= LD + LX, k < n + LD + LX))
        def _():
            rs_x2(k - LD - LX).start()
            rs_y2(k - LD - LX).start()

    def m_send(b):
        return send(xbuf.at[b], mpeer.at[b], ms.at[b], mr.at[b], zp)

    def out_send(b):
        return send(mpeer.at[b, :, mine], xbuf.at[b, :, mine], os_.at[b], or_.at[b], zp)

    def hid_send(u):
        i = u % 4
        return send(hown.at[i], hrecv.at[i], hs.at[i], hr.at[i], zp)

    for d in (z_q(0), z_k(0), z_v(0), z_o(0)):
        d.start()
    first = [pltpu.make_async_copy(x_ref, xbuf, wl.at[0])]
    for d in first:
        d.start()
    for d in first:
        d.wait()

    def first_rows(b, carry):
        hst[b % 2, 0] = _norm(xbuf[b], ga_ref[pl.ds(0, 1), :])
        d = h_store(ha.at[0], b, b % 2, 0)
        d.start()
        d.wait()
        ag_send_own(ha.at[0], sa, ra, b)
        return carry

    lax.fori_loop(0, NB, first_rows, 0)

    def first_forward(i, carry):
        ag_fwd1(ha.at[0], sa, ra, i)

        @pl.when(i >= 1)
        def _():
            ag_fwd2(ha.at[0], sa, ra, i - 1)

        return carry

    for ref, buf, sign in ((cos_ref, cbuf, 1.0), (sin_ref, sbuf, -1.0)):
        tab = ref[...].T
        tmp[...] = jnp.concatenate([sign * tab, tab], axis=1).reshape(4, 2, T, HD)
        buf[0] = tmp[:, c]
        buf[1] = tmp[:, 1 - c]

    lax.fori_loop(0, NB - 1, first_forward, 0)

    def when(*conds):
        c_ = conds[0]
        for d_ in conds[1:]:
            c_ = jnp.logical_and(c_, d_)
        return pl.when(c_)

    def pass_m(l, k):
        h = hb.at[l]

        def at(lag):
            if l == 0:
                q_ = k - lag - (NB + LT)
                return q_, jnp.logical_and(q_ >= 0, q_ < NB)
            q_ = k - lag - 5 - LT
            late = q_ > 8
            b_ = jnp.where(late, q_ - 4, q_ // 2)
            ok = jnp.logical_and(jnp.logical_and(q_ >= 0, q_ < 12), jnp.logical_or(late, q_ % 2 == 0))
            return b_, ok

        b0, ok0 = at(0)

        @pl.when(ok0)
        def _():
            hst[b0 % 2, 0] = _norm(xbuf[b0], gm_ref[pl.ds(l, 1), :])
            h_store(h, 2 * b0 + z, b0 % 2, 0).start()
            m_send(b0).start()

        b1, ok1 = at(1)

        @pl.when(ok1)
        def _():
            h_store(h, 2 * b1 + z, b1 % 2, 0).wait()
            ag_send_own(h, sb, rb, 2 * b1 + z)

        b3, ok3 = at(3)

        @pl.when(ok3)
        def _():
            h_store(h, 2 * b3 + 1 - z, b3 % 2, 1).wait()
            ag_send_own(h, sb, rb, 2 * b3 + 1 - z)

        b2, ok2 = at(2)

        @pl.when(ok2)
        def _():
            m_send(b2).wait()
            hst[b2 % 2, 1] = _norm(mpeer[b2], gm_ref[pl.ds(l, 1), :])
            h_store(h, 2 * b2 + 1 - z, b2 % 2, 1).start()

        b5, ok5 = at(5)

        @pl.when(ok5)
        def _():
            ag_fwd1(h, sb, rb, 2 * b5)
            ag_fwd1(h, sb, rb, 2 * b5 + 1)

        b7, ok7 = at(7)

        @pl.when(ok7)
        def _():
            ag_fwd2(h, sb, rb, 2 * b7)
            ag_fwd2(h, sb, rb, 2 * b7 + 1)

    def pass_y(l, s):
        @when(s >= 0, s < NU, s % 2 == 1 - z)
        def _():
            out_send(s // 2).start()

        last = l + 1 == n_layers

        @when(s >= 2, s < NU + 2, s % 2 == 0)
        def _():
            b = s // 2 - 1
            out_send(b).wait()
            if not last:
                hst[b % 2, 2] = _norm(xbuf[b], ga_ref[pl.ds(l + 1, 1), :])
                h_store(ha.at[l + 1], b, b % 2, 2).start()

        if not last:
            h = ha.at[l + 1]

            @when(s >= 3, s < NU + 3, s % 2 == 1)
            def _():
                b = s // 2 - 1
                h_store(h, b, b % 2, 2).wait()
                ag_send_own(h, sa, ra, b)

            @when(s >= 5, s < NU + 5, s % 2 == 1)
            def _():
                ag_fwd1(h, sa, ra, s // 2 - 2)

            @when(s >= 7, s < NU + 7, s % 2 == 1)
            def _():
                ag_fwd2(h, sa, ra, s // 2 - 3)

    def finish_y(s, low, high):
        b = s // 2
        ca = pl.ds(pl.multiple_of(z * W, 128), V)
        cb = pl.ds(pl.multiple_of(z * W + V, 128), V)

        @pl.when(s % 2 == z)
        def _():
            xbuf[b, :, ca] = (xbuf[b, :, ca].astype(F32) + low).astype(BF16)
            xbuf[b, :, cb] = (xbuf[b, :, cb].astype(F32) + high).astype(BF16)

        @pl.when(s % 2 == 1 - z)
        def _():
            mpeer[b, :, ca] = (mpeer[b, :, ca].astype(F32) + low).astype(BF16)
            mpeer[b, :, cb] = (mpeer[b, :, cb].astype(F32) + high).astype(BF16)

    def a_steps(l):
        return NU if l == 0 else NU + 1

    def a_unit(l, k):
        if l == 0:
            return k % NB, k, jnp.logical_and(k >= 0, k < NB), jnp.logical_and(k >= NB, k < NU)
        own = jnp.logical_and(k >= 0, jnp.logical_or(k < 3, jnp.logical_and(k % 2 == 0, k <= 12)))
        oth = jnp.logical_and(k >= 5, jnp.logical_or(jnp.logical_and(k % 2 == 1, k <= 13),
                                                     jnp.logical_and(k >= 14, k <= NU)))
        b_own = jnp.where(k < 3, k, (k + 2) // 2)
        b_oth = jnp.where(k < 14, (k - 5) // 2, k - 9)
        return jnp.where(own, b_own, b_oth), jnp.where(k < 4, k, k - 1), own, oth

    def a_stages(l, k):
        def at(lag):
            b, u, own, oth = a_unit(l, k - lag)
            return b, u, own, jnp.logical_or(own, oth)

        _, u2, _, ok2 = at(LD)
        pl.when(ok2)(lambda: rs_stage2(u2))
        _, u3, _, ok3 = at(LD + LX)
        pl.when(ok3)(lambda: rs_stage3(u3))
        b, u4, own4, ok4 = at(LT)

        @pl.when(ok4)
        def _():
            low, high = rs_stage4(u4)

            def add(col):
                ca = pl.ds(pl.multiple_of(col, 128), V)
                cb = pl.ds(pl.multiple_of(col + V, 128), V)
                xbuf[b, :, ca] = (xbuf[b, :, ca].astype(F32) + low).astype(BF16)
                xbuf[b, :, cb] = (xbuf[b, :, cb].astype(F32) + high).astype(BF16)

            pl.when(own4)(lambda: add(z * W))
            pl.when(jnp.logical_not(own4))(lambda: add((1 - z) * W))

    def a_sends(l, k):
        def at(lag):
            _, u, own, oth = a_unit(l, k - lag)
            return u, jnp.logical_or(own, oth)

        u1, ok1 = at(0)
        pl.when(ok1)(lambda: rs_d(u1).start())
        u2, ok2 = at(LD)

        @pl.when(ok2)
        def _():
            rs_x(u2).start()
            rs_y(u2).start()

        u3, ok3 = at(LD + LX)

        @pl.when(ok3)
        def _():
            rs_x2(u3).start()
            rs_y2(u3).start()

    def gap(l):
        return 8 if l == 0 else 2

    def b_steps(l):
        return gap(l) + LH + NU

    def pos_of(r):
        return 2 * T * ((r // T) % 4) + T * ((c + r // (4 * T)) % 2) + r % T

    def attend(l, k, b, h, wa_o, wa_r, wo_o, o_all):
        ag_finish(h, sa, ra, b)
        i = b % 2
        acc = jnp.dot(hv[i, :, :, :, mine].reshape(R, W), wa_o[...], preferred_element_type=F32)
        acc += jnp.dot(hv[i, :, :, :, other].reshape(R, W), wa_r[...], preferred_element_type=F32)
        qkv = acc.astype(BF16)
        cosv = cbuf[...].reshape(R, HD)
        sinv = sbuf[...].reshape(R, HD)

        def rope(t):
            t = t.astype(F32)
            return (t * cosv + pltpu.roll(t, HD // 2, 1) * sinv).astype(BF16)

        mask = pos_of(lax.broadcasted_iota(jnp.int32, (R, R), 0)) >= pos_of(
            lax.broadcasted_iota(jnp.int32, (R, R), 1))
        kk = rope(qkv[:, QW:QW + HD])
        vv = qkv[:, QW + HD:]
        for g in range(QW // HD):
            sc = lax.dot_general(rope(qkv[:, g * HD:(g + 1) * HD]), kk, NT, preferred_element_type=F32)
            sc = jnp.where(mask, sc * HD ** -0.5, -jnp.inf)
            e = jnp.exp(sc - jnp.max(sc, axis=-1, keepdims=True))
            p = (e / jnp.sum(e, axis=-1, keepdims=True)).astype(BF16)
            o_all[b, :, g * HD:(g + 1) * HD] = jnp.dot(p, vv, preferred_element_type=F32).astype(BF16)

    def loop_a(l, wa_o, wa_r, wo_o, wo_r, o_all):
        h = ha.at[l]
        loads = [pltpu.make_async_copy(wq_ref.at[l], wa_o.at[:, pl.ds(0, QW)], wl.at[0]),
                 pltpu.make_async_copy(wk_ref.at[l], wa_o.at[:, pl.ds(QW, HD)], wl.at[1]),
                 pltpu.make_async_copy(wv_ref.at[l], wa_o.at[:, pl.ds(QW + HD, HD)], wl.at[2]),
                 pltpu.make_async_copy(wo_ref.at[l], wo_o, wl.at[3])]
        for d in loads:
            d.start()
        ag_load(h, sa, ra, 0)
        for d in (z_q(l), z_k(l), z_v(l)):
            d.wait()
        more = [pltpu.make_async_copy(rq.at[l], wa_r.at[:, pl.ds(0, QW)], wl.at[4]),
                pltpu.make_async_copy(rk.at[l], wa_r.at[:, pl.ds(QW, HD)], wl.at[5]),
                pltpu.make_async_copy(rv.at[l], wa_r.at[:, pl.ds(QW + HD, HD)], wl.at[6])]
        for d in more:
            d.start()
        for d in loads + more:
            d.wait()
        first_other = NB if l == 0 else 5

        def step(k, carry):
            if l == 0:
                @pl.when(k == 0)
                def _():
                    ag_fwd1(h, sa, ra, NB - 1)

                @pl.when(k < 2)
                def _():
                    ag_fwd2(h, sa, ra, NB - 2 + k)

            b, u, own, oth = a_unit(l, k)

            @pl.when(own)
            def _():
                attend(l, k, b, h, wa_o, wa_r, wo_o, o_all)
                store_product(u, [(o_all[b], wo_o, None)])

            @pl.when(k == first_other)
            def _():
                z_o(l).wait()
                d = pltpu.make_async_copy(ro.at[l], wo_r, wl.at[7])
                d.start()
                d.wait()

            @pl.when(oth)
            def _():
                store_product(u, [(o_all[b], wo_r, None)])

            if l > 0:
                rs_steps(NU + k, NU, finish_y)
            a_stages(l, k)
            if l > 0:
                rs_sends(NU + k, NU)
            a_sends(l, k)
            if l > 0:
                pass_y(l - 1, NU + k - LT)
            pass_m(l, k)

            bn, _, own_next, _ = a_unit(l, k + 1)

            @pl.when(own_next)
            def _():
                ag_load(h, sa, ra, bn)

            if l == 0:
                @pl.when(k >= 8)
                def _():
                    z_gate_up_part(l, k - 8)
            else:
                @pl.when(k < 4)
                def _():
                    z_o_part(l, 4 + k)

                @when(k >= 4, k < 7)
                def _():
                    z_gate_up_part(l, 2 * (k - 4))
                    z_gate_up_part(l, 2 * (k - 4) + 1)

                @pl.when(k >= 7)
                def _():
                    z_gate_up_part(l, k - 1)

            return carry

        lax.fori_loop(0, a_steps(l), step, 0)

    def loop_b(l, g_o, g_r, u_o, u_r, wd_v):
        h = hb.at[l]
        mine_h = pl.ds(pl.multiple_of(z * HB, 16), HB)
        j0 = gap(l)
        loads = [pltpu.make_async_copy(wg_ref.at[l, mine_h], g_o, wl.at[0]),
                 pltpu.make_async_copy(wu_ref.at[l, mine_h], u_o, wl.at[1]),
                 pltpu.make_async_copy(wd_ref.at[l], wd_v, wl.at[2])]
        more = [pltpu.make_async_copy(rg.at[l], g_r, wl.at[3]),
                pltpu.make_async_copy(ru.at[l], u_r, wl.at[4])]
        for d in loads:
            d.start()

        def step(k, carry):
            @pl.when(k == j0)
            def _():
                for d in (z_g(l), z_u(l)):
                    d.wait()
                for d in more:
                    d.start()
                for d in loads + more:
                    d.wait()

            @when(k >= j0, k < j0 + NU)
            def _():
                u = k - j0
                ag_finish(h, sb, rb, u)
                i = u % 2
                hm = hv[i, :, :, :, mine].reshape(R, W)
                ho = hv[i, :, :, :, other].reshape(R, W)
                gate = lax.dot_general(hm, g_o[...], NT, preferred_element_type=F32)
                gate += lax.dot_general(ho, g_r[...], NT, preferred_element_type=F32)
                up = lax.dot_general(hm, u_o[...], NT, preferred_element_type=F32)
                up += lax.dot_general(ho, u_r[...], NT, preferred_element_type=F32)
                hown[u % 4] = (jax.nn.silu(gate) * up).astype(BF16)

            v = k - j0 - LH

            @pl.when(v >= 0)
            def _():
                hid_send(v).wait()
                store_product(v, [(hown[v % 4], wd_v, mine_h), (hrecv[v % 4], wd_v, theirs_h)])

            a_stages(l, a_steps(l) + k)
            rs_steps(v, NU, finish_y)

            @when(k >= j0, k < j0 + NU)
            def _():
                hid_send(k - j0).start()

            a_sends(l, a_steps(l) + k)
            rs_sends(v, NU)
            pass_m(l, a_steps(l) + k)
            pass_y(l, v - LT)

            @when(k >= j0 - 1, k < j0 + NU - 1)
            def _():
                ag_load(h, sb, rb, k - j0 + 1)

            if l == 0:
                @pl.when(k < 5)
                def _():
                    z_gate_up_part(l, 8 + k)

                @pl.when(k == 5)
                def _():
                    z_gate_up_part(l, 13)
                    z_gate_up_part(l, 14)

                @pl.when(k == 6)
                def _():
                    z_gate_up_part(l, 15)
                    z_gate_up_part(l, 16)
                    z_gate_up_part(l, 17)
            else:
                @pl.when(k < 2)
                def _():
                    z_gate_up_part(l, 16 + k)
            if l + 1 < n_layers:
                @pl.when(k == 7)
                def _():
                    z_qkv_part(l + 1, 0)

                @when(k >= 8, k <= 20, k % 2 == 0)
                def _():
                    z_qkv_part(l + 1, (k - 6) // 2)

                @pl.when(k >= 22)
                def _():
                    z_o_part(l + 1, k - 22)

            return carry

        lax.fori_loop(0, b_steps(l), step, 0)

    for l in range(n_layers):
        pl.run_scoped(
            functools.partial(loop_a, l),
            pltpu.VMEM((W, QW + 2 * HD), BF16), pltpu.VMEM((W, QW + 2 * HD), BF16),
            pltpu.VMEM((QW, W), BF16), pltpu.VMEM((QW, W), BF16), pltpu.VMEM((NB, R, QW), BF16))
        pl.run_scoped(
            functools.partial(loop_b, l),
            pltpu.VMEM((HB, W), BF16), pltpu.VMEM((HB, W), BF16),
            pltpu.VMEM((HB, W), BF16), pltpu.VMEM((HB, W), BF16), pltpu.VMEM((2 * HB, W), BF16))

    def tail(v, carry):
        rs_steps(v, NU, finish_y)
        rs_sends(v, NU)
        pass_y(n_layers - 1, v - LT)
        return carry

    lax.fori_loop(NU, NU + LT + 2, tail, 0)
    d = pltpu.make_async_copy(xbuf, y_ref, wl.at[0])
    d.start()
    d.wait()


def solution(mesh):
    act_spec = P("fsdp", "model", None)
    col_spec = P(None, "fsdp", "model")
    row_spec = P(None, "model", "fsdp")

    def device_step(x_in, gain_attn, gain_mlp, rope_cos, rope_sin, w_q, w_k, w_v, w_o, w_gate, w_up, w_down):
        L = w_q.shape[0]
        NB, T, D = x_in.shape
        W, V = D // 2, D // 4
        HB = w_gate.shape[2] // 2
        NU, R = 2 * NB, 8 * T
        half = rope_cos.shape[1]
        hbm = pl.BlockSpec(memory_space=pl.ANY)
        vmem = pl.BlockSpec(memory_space=pltpu.VMEM)
        dma = pltpu.SemaphoreType.DMA
        sds = jax.ShapeDtypeStruct
        outs = pl.pallas_call(
            _kernel,
            name="two_layers",
            in_specs=[hbm] + [vmem] * 4 + [hbm] * 7,
            out_specs=[hbm] * 9,
            out_shape=[
                sds(x_in.shape, BF16), sds(w_q.shape, BF16), sds(w_k.shape, BF16), sds(w_v.shape, BF16),
                sds(w_o.shape, BF16), sds((L, HB, W), BF16), sds((L, HB, W), BF16),
                sds((L, NB, 2, 4, T, D), BF16), sds((L, NU, 2, 4, T, D), BF16)],
            scratch_shapes=[
                pltpu.VMEM((NB, T, D), BF16), pltpu.VMEM((NB, T, D), BF16), pltpu.VMEM((2, 3, T, D), BF16),
                pltpu.VMEM((2, 2, 4, T, D), BF16),
                pltpu.VMEM((4, 2, 2, T, W), F32), pltpu.VMEM((2, 2, 2, T, W), F32), pltpu.VMEM((2, 2, 2, T, W), F32),
                pltpu.VMEM((4, 2, T, V), F32), pltpu.VMEM((4, 2, T, V), F32),
                pltpu.VMEM((4, 2, T, V), F32), pltpu.VMEM((4, 2, T, V), F32),
                pltpu.VMEM((4, T, V), F32), pltpu.VMEM((4, T, V), F32),
                pltpu.VMEM((4, R, HB), BF16), pltpu.VMEM((4, R, HB), BF16),
                pltpu.VMEM((2, 4, T, 2 * half), F32), pltpu.VMEM((2, 4, T, 2 * half), F32),
                pltpu.VMEM((4, 2, T, 2 * half), F32),
                dma((4,)), dma((4,)), dma((2,)), dma((2,)), dma((2,)), dma((2,)),
                dma((4,)), dma((4,)), dma((4,)), dma((4,)), dma((4,)), dma((4,)), dma((4,)), dma((4,)),
                dma((NB,)), dma((NB,)), dma((NB,)), dma((NB,)), dma((4,)), dma((4,)),
                dma((NB, 5)), dma((NB, 5)), dma((NU, 5)), dma((NU, 5)), dma((2, 3)), dma((2,)), dma((8,))],
            compiler_params=pltpu.CompilerParams(
                collective_id=0, has_side_effects=True, vmem_limit_bytes=67_000_000),
        )(x_in, gain_attn, gain_mlp, rope_cos.T, rope_sin.T, w_q, w_k, w_v, w_o,
          jnp.swapaxes(w_gate, 1, 2), jnp.swapaxes(w_up, 1, 2), w_down)
        return outs[0]

    return jax.shard_map(
        device_step, mesh=mesh,
        in_specs=(act_spec, P(), P(), P(), P(), col_spec, col_spec, col_spec, row_spec, col_spec, col_spec, row_spec),
        out_specs=act_spec, check_vma=False)
```

time: 1450 us -> 1310 us (0.903)
  Pallas kernels: 1440 us -> 1300 us
    pallas_call x1, Pallas kernels: 1440 us -> 1300 us  [device_step(): pl.pallas_call(_kernel, name='two_layers', in_specs=[hbm] + [vmem] * 4 +...]
where the time goes in v2:
time: 1310 us
  Pallas kernels  1300 us (99%)
    pallas_call x1, Pallas kernels, device_step(): pl.pallas_call(_kernel, name='two_layers', in_specs=[hbm] + [vmem] * 4 +...  1300 us

profile of v2, /device:TPU:0, one launch (start us, length us, event | category | flops | bytes accessed | tf_op | source)
XLA Modules:
  0.0 1305.4 jit_solution(1983925084158404766)
XLA Ops:
  0.0 1302.0 %two_layers.1 = (bf16[8,32,5120]{2,1,0:T(8,128)(2,1)}, bf16[2,2560,640]{2,1,0:T(8,128)(2,1)}, bf16[2,2560,128]{2,1,0:T(8,128)(2,1)}, bf16[2,2560,128]{2,1,0:T(8,...) custom-call(bf16[8,32,5120]{2,1,0:T(8,128)(2,1)} %x_ref.1, ...), custom_call_target="tpu_custom_call" | custom-call | tf_op jit(solution)/shard_map/two_layers/pallas_call | solution.py:693
  1302.0 3.4 copy.14

commit v3 on v2

v3 whole, which is shorter than its diff:
```python
import functools

import jax
import jax.numpy as jnp
from jax import lax
from jax.experimental import pallas as pl
from jax.experimental.pallas import tpu as pltpu
from jax.sharding import PartitionSpec as P

EPS = 1e-5
MESH = pl.DeviceIdType.MESH
NN = (((1,), (0,)), ((), ()))
NT = (((1,), (1,)), ((), ()))
TN = (((0,), (0,)), ((), ()))
LD = 1
LX = 2
LT = LD + 2 * LX
LH = 2
LM = (2, 2)
GAP = (8, 6)
SLOTS, CHIPS, CORES, PAIR = 4, 4, 2, 2
ALIGN, LANES = 16, 128
SEMS = "442222444444448888444433" + "22888"
GU, ATTN = 9, 8

CUT_A = (20, 38)
CUT_B = (22, 16)
CUTS = 40

ATTEND = ("01234567--------", "012-3-4-5-6-7-------")
OWN = ("01234567--------", "--012-3-4-5-6-7-----")
OTHER = ("--------01234567", "---------0-1-2-34567")
GU_IN_A = ("0000001111111111", "00010220211000111111")
GU_IN_B = ("111122", "1011")
QKV_IN_B = ("000000011010101010101", "")
O_IN_A = ("", "1211")
O_IN_B = ("00000000000000000000000012", "")
F32 = jnp.float32
BF16 = jnp.bfloat16


def _norm(rows, gain):
    rows = rows.astype(F32)
    mean_sq = jnp.mean(rows * rows, axis=-1, keepdims=True)
    return (rows * lax.rsqrt(mean_sq + EPS) * gain).astype(BF16)


def _kernel(
    x_ref, ga_ref, gm_ref, cos_ref, sin_ref, wq_ref, wk_ref, wv_ref, wo_ref, wg_ref, wu_ref, wd_ref,
    y_ref, rq, rk, rv, ro, rg, ru, ha, hb, rw, row,
    xbuf, mpeer, hst, hv, pown, psib, rd, t1, t2, rx, ry, rx2, ry2, hown, hrecv, cbuf, sbuf, tmp, ox, xres, mst,
    zs, zr, gs, gr, ds, dr, xs, xr, ys, yr, x2s, x2r, y2s, y2r, ms, mr, os_, or_, hs, hr, mxs, mxr, wxs, wxr,
    loc, hvs, wl, oxs, oxr, sa, ra, sb, rb, xrs, xrr,
):
    n_layers = wq_ref.shape[0]
    NB, T, D = x_ref.shape
    W, V = D // PAIR, D // CHIPS
    QW = wq_ref.shape[2]
    HD = wk_ref.shape[2]
    HB = wg_ref.shape[1] // PAIR
    R = CHIPS * CORES * T
    NU = PAIR * NB

    z = lax.axis_index("fsdp")
    m = lax.axis_index("model")
    y, x, c, q = m // 4, (m // 2) % 2, m % 2, m // 2
    qx, qy, qd = q + 1 - 2 * x, q + 2 - 4 * y, 3 - q
    zp, xp, yp, sp = (1 - z, m), (z, m + 2 - 4 * x), (z, m + 4 - 8 * y), (z, m + 1 - 2 * c)

    def lanes(start, size):
        return pl.ds(pl.multiple_of(start, LANES), size)

    def rows(start, size):
        return pl.ds(pl.multiple_of(start, ALIGN), size)

    mine, other = lanes(z * W, W), lanes((1 - z) * W, W)
    low_v, high_v = pl.ds(0, V), pl.ds(V, V)

    def even(i):
        return i % PAIR == 0

    def half_of(i):
        return i // PAIR

    def when(*conds):
        return pl.when(functools.reduce(jnp.logical_and, conds))

    def within(k, n):
        return jnp.logical_and(k >= 0, k < n)

    def lookup(table, k):
        runs = []
        for i in sorted(table):
            if runs:
                run = runs[-1]
                stride = i - run[-1]
                if table[i] == table[run[-1]] + 1 and stride in (1, PAIR) and (
                        len(run) == 1 or stride == run[-1] - run[-2]):
                    run.append(i)
                    continue
            runs.append([i])
        value, there = None, None
        for run in reversed(runs):
            first, last = run[0], run[-1]
            stride = run[1] - first if len(run) > 1 else 1
            ok = jnp.logical_and(k >= first, k <= last)
            if stride > 1:
                ok = jnp.logical_and(ok, (k - first) % stride == 0)
            val = (k - first) // stride + table[first]
            value = val if value is None else jnp.where(k <= last, val, value)
            there = ok if there is None else jnp.logical_or(there, ok)
        return value, there

    def table(text):
        return {i: int(ch) for i, ch in enumerate(text) if ch.isdigit()}

    def parts(texts, k, start):
        done = sum(int(ch) for text in texts[:-1] for ch in text)
        for i, ch in enumerate(texts[-1]):
            n = int(ch)
            if n:
                @pl.when(k == i)
                def _():
                    for j in range(done, done + n):
                        start(j)
            done += n

    barrier = pltpu.get_barrier_semaphore()
    for dev in (zp, xp, yp, sp):
        pl.semaphore_signal(barrier, inc=1, device_id=dev, device_id_type=MESH)
    pl.semaphore_wait(barrier, 4)

    def send(src, dst, s, r, dev):
        return pltpu.make_async_remote_copy(
            src_ref=src, dst_ref=dst, send_sem=s, recv_sem=r, device_id=dev, device_id_type=MESH)

    def z_q(l):
        return send(wq_ref.at[l], rq.at[l], zs.at[0], zr.at[0], zp)

    def z_k(l):
        return send(wk_ref.at[l], rk.at[l], zs.at[1], zr.at[1], zp)

    def z_v(l):
        return send(wv_ref.at[l], rv.at[l], zs.at[2], zr.at[2], zp)

    def z_o(l):
        return send(wo_ref.at[l], ro, zs.at[3], zr.at[3], zp)

    mine_h, theirs_h = rows(z * HB, HB), rows((1 - z) * HB, HB)

    def z_g(l):
        return send(wg_ref.at[l, theirs_h], rg.at[l], gs.at[0], gr.at[0], zp)

    def z_u(l):
        return send(wu_ref.at[l, theirs_h], ru.at[l], gs.at[1], gr.at[1], zp)

    def z_gate_up_part(l, j):
        size = HB // GU
        ref, out, i = (wg_ref, rg, 0) if j < GU else (wu_ref, ru, 1)
        at = (j % GU) * size
        send(ref.at[l, rows((1 - z) * HB + at, size)], out.at[l, pl.ds(at, size)], gs.at[i], gr.at[i], zp).start()

    def z_qkv_part(l, j):
        size = W // ATTN
        at = pl.ds(j * size, size)
        for i, (ref, out) in enumerate(((wq_ref, rq), (wk_ref, rk), (wv_ref, rv))):
            send(ref.at[l, at], out.at[l, at], zs.at[i], zr.at[i], zp).start()

    def z_o_part(l, j):
        size = QW // ATTN
        for d in z_oq(l, pl.ds(j * size, size)):
            d.start()

    def cut_of(share):
        return max(1, D // LANES * share // CUTS) * LANES

    def cut_a(l):
        return cut_of(CUT_A[l])

    def cut_b(l):
        return cut_of(CUT_B[l])

    def ag_own(h, s, r, u):
        own = h.at[u, 0, q]
        return [send(own, own, s.at[u, i], r.at[u, i], dev) for i, dev in enumerate((xp, yp))]

    def ag_fwd(h, s, r, u, cut):
        from_x, from_y = h.at[u, 0, qx, :, pl.ds(0, cut)], h.at[u, 0, qy, :, pl.ds(cut, D - cut)]
        return [send(from_x, from_x, s.at[u, 2], r.at[u, 2], yp), send(from_y, from_y, s.at[u, 3], r.at[u, 3], xp)]

    def ag_sib(h, s, r, u):
        return send(h.at[u, 0], h.at[u, 1], s.at[u, CHIPS], r.at[u, CHIPS], sp)

    def ag_send_own(h, s, r, u):
        for d in ag_own(h, s, r, u):
            d.start()

    def ag_fwd1(h, s, r, u, cut):
        for own, fwd in zip(ag_own(h, s, r, u), ag_fwd(h, s, r, u, cut)):
            own.wait_recv()
            fwd.start()

    def ag_fwd2(h, s, r, u, cut):
        for fwd in ag_fwd(h, s, r, u, cut):
            fwd.wait_recv()
        ag_sib(h, s, r, u).start()

    def ag_local(h, u):
        return pltpu.make_async_copy(h.at[u], hv.at[u % PAIR], hvs.at[u % PAIR])

    def ag_load(h, s, r, u):
        ag_sib(h, s, r, u).wait_recv()
        ag_local(h, u).start()

    def ag_finish(h, s, r, u, cut):
        ag_local(h, u).wait()
        for d in ag_own(h, s, r, u) + ag_fwd(h, s, r, u, cut) + [ag_sib(h, s, r, u)]:
            d.wait_send()

    def y_store(b):
        return pltpu.make_async_copy(xbuf.at[b], y_ref.at[b], oxs.at[b])

    def h_store(h, u, j):
        return pltpu.make_async_copy(hst.at[j], h.at[u, 0, q], loc.at[j])

    def rs_d(u):
        return send(psib.at[u % PAIR], rd.at[u % PAIR], ds.at[u % PAIR], dr.at[u % PAIR], sp)

    def rs_x(u):
        i = u % SLOTS
        return send(pown.at[i, :, 1 - x, :, low_v], rx.at[i], xs.at[i], xr.at[i], xp)

    def rs_y(u):
        i = u % SLOTS
        return send(pown.at[i, 1 - y, :, :, high_v], ry.at[i], ys.at[i], yr.at[i], yp)

    def ra_d(u):
        return send(psib.at[u % PAIR, :, :, :, low_v], rd.at[u % PAIR, :, :, :, low_v],
                    ds.at[u % PAIR], dr.at[u % PAIR], sp)

    def ra_y(u):
        i = u % SLOTS
        return send(pown.at[i, 1 - y, :, :, low_v], ry.at[i], ys.at[i], yr.at[i], yp)

    def ra_m(u, b, half):
        cols = lanes(half * W + x * V, V)
        return send(mst.at[u % (LH + 1)], xbuf.at[b, :, cols], mxs.at[u % SLOTS], mxr.at[u % SLOTS], xp)

    def o_send(o_all, b):
        return send(o_all.at[b], ox.at[b % (NB - 1)], oxs.at[b], oxr.at[b], xp)

    def res_send(b, half):
        src = lanes(half * W + (1 - x) * V, V)
        dst = lanes(half * V, V)
        return send(xbuf.at[b, :, src], xres.at[b, :, dst], xrs.at[b, half], xrr.at[b, half], xp)

    def w_send(l):
        cols = lanes((1 - x) * V, V)
        return send(wo_ref.at[l, :, cols], rw.at[...], wxs.at[0], wxr.at[0], xp)

    def z_oq(l, rows=slice(None)):
        cols = lanes(x * V, V)
        return (send(wo_ref.at[l, rows, cols], row.at[0, rows], wxs.at[1], wxr.at[1], zp),
                send(rw.at[rows], row.at[1, rows], wxs.at[2], wxr.at[2], zp))

    def rs_x2(u):
        i = u % SLOTS
        return send(t2.at[u % (LH + 1), 1 - x], rx2.at[i], x2s.at[i], x2r.at[i], xp)

    def rs_y2(u):
        i = u % SLOTS
        return send(t1.at[u % (LH + 1), 1 - y], ry2.at[i], y2s.at[i], y2r.at[i], yp)

    def store_product(u, pairs, width):
        half = W // 2
        for j in range(width // half):
            cols = pl.ds(j * half, half)
            acc = None
            for a, w, rows in pairs:
                wv_ = w[:, cols] if rows is None else w[rows, cols]
                p = lax.dot_general(a, wv_, TN if rows is not None else NN, preferred_element_type=F32)
                acc = p if acc is None else acc + p
            pown[u % SLOTS, :, :, :, cols] = acc[: R // 2].reshape(2, 2, T, half)
            psib[u % PAIR, :, :, :, cols] = acc[R // 2:].reshape(2, 2, T, half)

    def rs_stage2(u):
        rs_d(u).wait()
        pown[u % SLOTS] = pown[u % SLOTS] + rd[u % PAIR]

    def rs_stage3(u):
        i = u % SLOTS
        rs_x(u).wait()
        rs_y(u).wait()
        t1[u % (LH + 1)] = pown[i, :, x, :, low_v] + rx[i]
        t2[u % (LH + 1)] = pown[i, y, :, :, high_v] + ry[i]

    def rs_stage4(u):
        i = u % SLOTS
        rs_x2(u).wait()
        rs_y2(u).wait()
        return t1[u % (LH + 1), y] + ry2[i], t2[u % (LH + 1), x] + rx2[i]

    def rs_steps(k, n, finish):
        @pl.when(jnp.logical_and(k >= LD, k < n + LD))
        def _():
            rs_stage2(k - LD)

        @pl.when(jnp.logical_and(k >= LD + LX, k < n + LD + LX))
        def _():
            rs_stage3(k - LD - LX)

        @pl.when(jnp.logical_and(k >= LT, k < n + LT))
        def _():
            finish(k - LT, *rs_stage4(k - LT))

    def rs_sends(k, n):
        @pl.when(jnp.logical_and(k >= 0, k < n))
        def _():
            rs_d(k).start()

        @pl.when(jnp.logical_and(k >= LD, k < n + LD))
        def _():
            rs_x(k - LD).start()
            rs_y(k - LD).start()

        @pl.when(jnp.logical_and(k >= LD + LX, k < n + LD + LX))
        def _():
            rs_x2(k - LD - LX).start()
            rs_y2(k - LD - LX).start()

    def m_send(b):
        return send(xbuf.at[b], mpeer.at[b], ms.at[b], mr.at[b], zp)

    def out_send(b):
        return send(mpeer.at[b, :, mine], xbuf.at[b, :, mine], os_.at[b], or_.at[b], zp)

    def hid_send(u):
        i = u % SLOTS
        return send(hown.at[u % (LH + 1)], hrecv.at[i], hs.at[i], hr.at[i], zp)

    for d in (z_q(0), z_k(0), z_v(0), z_o(0)):
        d.start()
    first = [pltpu.make_async_copy(x_ref, xbuf, wl.at[0])]
    for d in first:
        d.start()
    for d in first:
        d.wait()

    def first_rows(b, carry):
        hst[0] = _norm(xbuf[b], ga_ref[pl.ds(0, 1), :])
        d = h_store(ha.at[0], b, 0)
        d.start()
        d.wait()
        ag_send_own(ha.at[0], sa, ra, b)
        return carry

    lax.fori_loop(0, NB, first_rows, 0)

    def first_forward(i, carry):
        ag_fwd1(ha.at[0], sa, ra, i, cut_a(0))

        @pl.when(i >= 1)
        def _():
            ag_fwd2(ha.at[0], sa, ra, i - 1, cut_a(0))

        return carry

    for ref, buf, sign in ((cos_ref, cbuf, 1.0), (sin_ref, sbuf, -1.0)):
        tab = ref[...].T
        tmp[...] = jnp.concatenate([sign * tab, tab], axis=1).reshape(4, 2, T, HD)
        buf[0] = tmp[:, c]
        buf[1] = tmp[:, 1 - c]

    lax.fori_loop(0, NB, first_forward, 0)
    w_send(1).start()
    def pass_m(l, k):
        h = hb.at[l]
        cut = cut_b(l)
        wait_m = LM[l]

        def at(lag, run):
            b, ok = lookup(table(OTHER[l]), k - lag - LT)
            pl.when(ok)(lambda: run(b))

        def own(b):
            return PAIR * b + z

        def theirs(b):
            return PAIR * b + 1 - z

        def send_own(b):
            h_store(h, own(b), 0).wait()
            ag_send_own(h, sb, rb, own(b))

        def start_own(b):
            hst[0] = _norm(xbuf[b], gm_ref[pl.ds(l, 1), :])
            h_store(h, own(b), 0).start()
            m_send(b).start()

        def send_theirs(b):
            h_store(h, theirs(b), 1).wait()
            ag_send_own(h, sb, rb, theirs(b))

        def start_theirs(b):
            m_send(b).wait()
            hst[1] = _norm(mpeer[b], gm_ref[pl.ds(l, 1), :])
            h_store(h, theirs(b), 1).start()

        def forward(b):
            for j in range(PAIR):
                ag_fwd1(h, sb, rb, PAIR * b + j, cut)

        def forward_more(b):
            for j in range(PAIR):
                ag_fwd2(h, sb, rb, PAIR * b + j, cut)

        at(1, send_own)
        at(0, start_own)
        at(wait_m + 1, send_theirs)
        at(wait_m, start_theirs)
        at(wait_m + LX + 1, forward)
        at(wait_m + LX + LX + 1, forward_more)

    def pass_y(l, s):
        last = l + 1 == n_layers

        @when(within(s, NU), s % PAIR == 1 - z)
        def _():
            out_send(half_of(s)).start()

        def at(lag, run):
            i = s - lag - 1
            when(within(i, NU), even(i))(lambda: run(half_of(i)))

        def got(b):
            out_send(b).wait()
            if last:
                y_store(b).start()
                return
            hst[0] = _norm(xbuf[b], ga_ref[pl.ds(l + 1, 1), :])
            h_store(ha.at[l + 1], b, 0).start()
            for half in range(PAIR):
                res_send(b, half).start()

        at(1, got)
        if not last:
            h, cut = ha.at[l + 1], cut_a(l + 1)

            def send_own(b):
                h_store(h, b, 0).wait()
                ag_send_own(h, sa, ra, b)

            at(LX, send_own)
            at(LX + LX, lambda b: ag_fwd1(h, sa, ra, b, cut))
            at(LX + LX + LX, lambda b: ag_fwd2(h, sa, ra, b, cut))

    def add(buf, b, start, low, high):
        for at, part in ((start, low), (start + V, high)):
            cols = lanes(at, V)
            buf[b, :, cols] = (buf[b, :, cols].astype(F32) + part).astype(BF16)

    def finish_y(s, low, high):
        b = half_of(s)
        pl.when(s % PAIR == z)(lambda: add(xbuf, b, z * W, low, high))
        pl.when(s % PAIR == 1 - z)(lambda: add(mpeer, b, z * W, low, high))

    def finish_m(u, low, high):
        half = z + (u // NB) * (1 - z - z)
        add(xbuf, u % NB, half * W, low, high)

    def a_steps(l):
        return len(ATTEND[l])

    def a_attend(l, k):
        return lookup(table(ATTEND[l]), k)

    def a_unit(l, k):
        own, oth = table(OWN[l]), table(OTHER[l])
        b_own, is_own = lookup(own, k)
        b_oth, is_oth = lookup(oth, k)
        u, _ = lookup({i: n for n, i in enumerate(sorted({**own, **oth}))}, k)
        return jnp.where(is_own, b_own, b_oth), u, is_own, is_oth

    def a_stages(l, k):
        if l == 0:
            rs_steps(k, NU, finish_m)
            return

        def at(lag):
            b, u, own, oth = a_unit(l, k - lag)
            half = jnp.where(own, z, 1 - z)
            return b, u, half, jnp.logical_or(own, oth)

        _, u2, _, ok2 = at(LD)

        @pl.when(ok2)
        def _():
            ra_d(u2).wait()
            cols = low_v
            pown[u2 % SLOTS, :, :, :, cols] = pown[u2 % SLOTS, :, :, :, cols] + rd[u2 % PAIR, :, :, :, cols]

        b3, u3, half3, ok3 = at(LD + LX)

        @pl.when(ok3)
        def _():
            i = u3 % SLOTS
            ra_y(u3).wait()
            res_send(b3, half3).wait_recv()
            cols = lanes(half3 * W + x * V, V)
            xbuf[b3, :, cols] = (xbuf[b3, :, cols].astype(F32)
                                 + (pown[i, y, x, :, low_v] + ry[i, x])).astype(BF16)
            res = xres[b3, :, lanes(half3 * V, V)].astype(F32)
            mst[u3 % (LH + 1)] = (res + (pown[i, y, 1 - x, :, low_v] + ry[i, 1 - x])).astype(BF16)

        b4, u4, half4, ok4 = at(LT)
        pl.when(ok4)(lambda: ra_m(u4, b4, half4).wait())

    def a_sends(l, k):
        if l == 0:
            rs_sends(k, NU)
            return

        def at(lag):
            b, u, own, oth = a_unit(l, k - lag)
            return b, u, jnp.where(own, z, 1 - z), jnp.logical_or(own, oth)

        _, u1, _, ok1 = at(0)
        pl.when(ok1)(lambda: ra_d(u1).start())
        _, u2, _, ok2 = at(LD)
        pl.when(ok2)(lambda: ra_y(u2).start())
        b3, u3, half3, ok3 = at(LD + LX)
        pl.when(ok3)(lambda: ra_m(u3, b3, half3).start())

    def b_steps(l):
        return GAP[l] + LH + NU

    def pos_of(r):
        rail = r // (CHIPS * T)
        return CORES * T * ((r // T) % CHIPS) + T * ((c + rail) % CORES) + r % T

    def attend(l, b, h, wa_o, wa_r, o_all):
        ag_finish(h, sa, ra, b, cut_a(l))
        i = b % PAIR
        acc = jnp.dot(hv[i, :, :, :, mine].reshape(R, W), wa_o[...], preferred_element_type=F32)
        acc += jnp.dot(hv[i, :, :, :, other].reshape(R, W), wa_r[...], preferred_element_type=F32)
        qkv = acc.astype(BF16)
        cosv = cbuf[...].reshape(R, HD)
        sinv = sbuf[...].reshape(R, HD)

        def rope(t):
            t = t.astype(F32)
            return (t * cosv + pltpu.roll(t, HD // 2, 1) * sinv).astype(BF16)

        mask = pos_of(lax.broadcasted_iota(jnp.int32, (R, R), 0)) >= pos_of(
            lax.broadcasted_iota(jnp.int32, (R, R), 1))
        kk = rope(qkv[:, QW:QW + HD])
        vv = qkv[:, QW + HD:]
        for g in range(QW // HD):
            sc = lax.dot_general(rope(qkv[:, g * HD:(g + 1) * HD]), kk, NT, preferred_element_type=F32)
            sc = jnp.where(mask, sc * HD ** -0.5, -jnp.inf)
            e = jnp.exp(sc - jnp.max(sc, axis=-1, keepdims=True))
            p = (e / jnp.sum(e, axis=-1, keepdims=True)).astype(BF16)
            o_all[b, :, g * HD:(g + 1) * HD] = jnp.dot(p, vv, preferred_element_type=F32).astype(BF16)

    def loop_a(l, wa_o, wa_r, w_own, w_oth, o_all):
        h = ha.at[l]
        my_v = lanes(x * V, V)
        loads = [pltpu.make_async_copy(wq_ref.at[l], wa_o.at[:, pl.ds(0, QW)], wl.at[0]),
                 pltpu.make_async_copy(wk_ref.at[l], wa_o.at[:, pl.ds(QW, HD)], wl.at[1]),
                 pltpu.make_async_copy(wv_ref.at[l], wa_o.at[:, pl.ds(QW + HD, HD)], wl.at[2]),
                 pltpu.make_async_copy(wo_ref.at[l] if l == 0 else wo_ref.at[l, :, my_v],
                                       w_own.at[0], wl.at[3])]
        if l > 0:
            loads.append(pltpu.make_async_copy(rw, w_own.at[1], wl.at[7]))
        for d in loads:
            d.start()
        ag_load(h, sa, ra, 0)
        for d in (z_q(l), z_k(l), z_v(l)):
            d.wait()
        more = [pltpu.make_async_copy(rq.at[l], wa_r.at[:, pl.ds(0, QW)], wl.at[4]),
                pltpu.make_async_copy(rk.at[l], wa_r.at[:, pl.ds(QW, HD)], wl.at[5]),
                pltpu.make_async_copy(rv.at[l], wa_r.at[:, pl.ds(QW + HD, HD)], wl.at[6])]
        for d in more:
            d.start()
        for d in loads + more:
            d.wait()
        first_other = min(table(OTHER[l]))

        def step(k, carry):
            if l == 0:
                @pl.when(k == 0)
                def _():
                    ag_fwd2(h, sa, ra, NB - 1, cut_a(0))

            bn, next_ok = a_attend(l, k + 1)
            pl.when(next_ok)(lambda: ag_load(h, sa, ra, bn))
            ba, ok = a_attend(l, k)
            pl.when(ok)(lambda: attend(l, ba, h, wa_o, wa_r, o_all))
            b, u, own, oth = a_unit(l, k)

            @pl.when(own)
            def _():
                if l == 0:
                    store_product(u, [(o_all[b], w_own.at[0], None)], W)
                else:
                    o_send(o_all, b).wait()
                    store_product(u, [(o_all[b], w_own.at[0], None), (ox[b % (NB - 1)], w_own.at[1], None)], V)

            @pl.when(k == first_other)
            def _():
                got = (z_o(l),) if l == 0 else z_oq(l)
                for d in got:
                    d.wait()
                if l == 0:
                    into = [pltpu.make_async_copy(ro, w_oth.at[0], wl.at[5])]
                else:
                    into = [pltpu.make_async_copy(row.at[i], w_oth.at[i], wl.at[5 + i]) for i in range(2)]
                for d in into:
                    d.start()
                for d in into:
                    d.wait()

            @pl.when(oth)
            def _():
                if l == 0:
                    store_product(u, [(o_all[b], w_oth.at[0], None)], W)
                else:
                    store_product(u, [(o_all[b], w_oth.at[0], None), (ox[b % (NB - 1)], w_oth.at[1], None)], V)

            if l > 0:
                rs_steps(NU + k, NU, finish_y)
            a_stages(l, k)
            if l > 0:
                rs_sends(NU + k, NU)
            if l > 0:
                @pl.when(ok)
                def _():
                    for half in range(2):
                        res_send(ba, half).wait_send()
                    o_send(o_all, ba).start()

            a_sends(l, k)
            if l > 0:
                pass_y(l - 1, NU + k - LT)
            pass_m(l, k)

            parts((O_IN_B[l - 1], O_IN_A[l]), k, functools.partial(z_o_part, l))
            parts((GU_IN_A[l],), k, functools.partial(z_gate_up_part, l))
            return carry

        lax.fori_loop(0, a_steps(l), step, 0)

    def loop_b(l, g_o, g_r, u_o, u_r, wd_v):
        h = hb.at[l]
        j0 = GAP[l]
        loads = [pltpu.make_async_copy(wg_ref.at[l, mine_h], g_o, wl.at[0]),
                 pltpu.make_async_copy(wu_ref.at[l, mine_h], u_o, wl.at[1]),
                 pltpu.make_async_copy(wd_ref.at[l], wd_v, wl.at[2])]
        more = [pltpu.make_async_copy(rg.at[l], g_r, wl.at[3]),
                pltpu.make_async_copy(ru.at[l], u_r, wl.at[4])]
        for d in loads:
            d.start()

        def step(k, carry):
            @pl.when(k == j0)
            def _():
                for d in (z_g(l), z_u(l)):
                    d.wait()
                for d in more:
                    d.start()
                for d in loads + more:
                    d.wait()

            @when(k >= j0 - 1, k < j0 + NU - 1)
            def _():
                ag_load(h, sb, rb, k - j0 + 1)

            @when(k >= j0, k < j0 + NU)
            def _():
                u = k - j0
                ag_finish(h, sb, rb, u, cut_b(l))
                i = u % PAIR
                hm = hv[i, :, :, :, mine].reshape(R, W)
                ho = hv[i, :, :, :, other].reshape(R, W)
                gate = lax.dot_general(g_o[...], hm, NT, preferred_element_type=F32)
                gate += lax.dot_general(g_r[...], ho, NT, preferred_element_type=F32)
                up = lax.dot_general(u_o[...], hm, NT, preferred_element_type=F32)
                up += lax.dot_general(u_r[...], ho, NT, preferred_element_type=F32)
                hown[u % (LH + 1)] = (jax.nn.silu(gate) * up).astype(BF16)

            v = k - j0 - LH

            @pl.when(v >= 0)
            def _():
                hid_send(v).wait()
                store_product(v, [(hown[v % (LH + 1)], wd_v, mine_h), (hrecv[v % SLOTS], wd_v, theirs_h)], W)

            a_stages(l, a_steps(l) + k)
            rs_steps(v, NU, finish_y)

            @when(k >= j0, k < j0 + NU)
            def _():
                hid_send(k - j0).start()

            a_sends(l, a_steps(l) + k)
            rs_sends(v, NU)
            pass_m(l, a_steps(l) + k)
            pass_y(l, v - LT)

            parts((GU_IN_A[l], GU_IN_B[l]), k, functools.partial(z_gate_up_part, l))
            if l + 1 < n_layers:
                @pl.when(k == min(table(O_IN_B[l].replace("0", "-"))))
                def _():
                    w_send(l + 1).wait()

                parts((QKV_IN_B[l],), k, functools.partial(z_qkv_part, l + 1))
                parts((O_IN_B[l],), k, functools.partial(z_o_part, l + 1))

            return carry

        lax.fori_loop(0, b_steps(l), step, 0)

    for l in range(n_layers):
        pl.run_scoped(
            functools.partial(loop_a, l),
            pltpu.VMEM((W, QW + 2 * HD), BF16), pltpu.VMEM((W, QW + 2 * HD), BF16),
            pltpu.VMEM((1, QW, W) if l == 0 else (2, QW, V), BF16),
            pltpu.VMEM((1, QW, W) if l == 0 else (2, QW, V), BF16), pltpu.VMEM((NB, R, QW), BF16))
        pl.run_scoped(
            functools.partial(loop_b, l),
            pltpu.VMEM((HB, W), BF16), pltpu.VMEM((HB, W), BF16),
            pltpu.VMEM((HB, W), BF16), pltpu.VMEM((HB, W), BF16), pltpu.VMEM((2 * HB, W), BF16))

    def tail(v, carry):
        rs_steps(v, NU, finish_y)
        rs_sends(v, NU)
        pass_y(n_layers - 1, v - LT)
        return carry

    lax.fori_loop(NU, NU + LT + 2, tail, 0)
    for b in range(NB):
        y_store(b).wait()


def solution(mesh):
    act_spec = P("fsdp", "model", None)
    col_spec = P(None, "fsdp", "model")
    row_spec = P(None, "model", "fsdp")

    def device_step(x_in, gain_attn, gain_mlp, rope_cos, rope_sin, w_q, w_k, w_v, w_o, w_gate, w_up, w_down):
        L, NB, T, D = w_q.shape[0], *x_in.shape
        W, V = D // PAIR, D // CHIPS
        HB = w_gate.shape[-1] // PAIR
        NU, R = PAIR * NB, CHIPS * CORES * T
        HD = PAIR * rope_cos.shape[-1]
        QW = w_o.shape[1]
        hbm = pl.BlockSpec(memory_space=pl.ANY)
        vmem = pl.BlockSpec(memory_space=pltpu.VMEM)
        sds = jax.ShapeDtypeStruct

        def buf(dtype, *shape):
            return pltpu.VMEM(shape, dtype)

        def sems(*shape):
            return pltpu.SemaphoreType.DMA(shape)

        args = (x_in, gain_attn, gain_mlp, rope_cos.T, rope_sin.T, w_q, w_k, w_v, w_o,
                jnp.swapaxes(w_gate, 1, -1), jnp.swapaxes(w_up, 1, -1), w_down)
        half_rows, plane_rows = (L, HB, W), (CORES, CHIPS, T, D)
        shapes = [x_in.shape, w_q.shape, w_k.shape, w_v.shape, w_o.shape[1:], half_rows, half_rows,
                  (L, NB) + plane_rows, (L, NU) + plane_rows, (QW, V), (PAIR, QW, V)]
        unit, hop = (PAIR, PAIR, T, W), (PAIR, T, V)
        in_flight, hidden, tables = LH + 1, (HB, R), (CORES, CHIPS, T, HD)
        outs = pl.pallas_call(
            _kernel,
            name="two_layers",
            in_specs=[vmem if a.ndim <= PAIR else hbm for a in args],
            out_specs=[hbm] * len(shapes),
            out_shape=[sds(shape, BF16) for shape in shapes],
            scratch_shapes=[
                buf(BF16, NB, T, D), buf(BF16, NB, T, D), buf(BF16, PAIR, T, D), buf(BF16, PAIR, *plane_rows),
                buf(F32, SLOTS, *unit), buf(F32, PAIR, *unit), buf(F32, PAIR, *unit),
                buf(F32, in_flight, *hop), buf(F32, in_flight, *hop), buf(F32, SLOTS, *hop), buf(F32, SLOTS, *hop),
                buf(F32, SLOTS, T, V), buf(F32, SLOTS, T, V), buf(BF16, in_flight, *hidden), buf(BF16, SLOTS, *hidden),
                buf(F32, *tables), buf(F32, *tables), buf(F32, CHIPS, CORES, T, HD),
                buf(BF16, NB - 1, R, QW), buf(BF16, NB, T, W), buf(BF16, in_flight, T, V)]
            + [sems(int(ch)) for ch in SEMS] + [sems(NB, CHIPS + 1), sems(NB, CHIPS + 1), sems(NU, CHIPS + 1),
                                                sems(NU, CHIPS + 1), sems(NB, PAIR), sems(NB, PAIR)],
            compiler_params=pltpu.CompilerParams(
                collective_id=0, has_side_effects=True, vmem_limit_bytes=67_000_000),
        )(*args)
        return outs[0]

    return jax.shard_map(
        device_step, mesh=mesh,
        in_specs=(act_spec, P(), P(), P(), P(), col_spec, col_spec, col_spec, row_spec, col_spec, col_spec, row_spec),
        out_specs=act_spec, check_vma=False)
```

time: 1310 us -> 1250 us (0.954)
  Pallas kernels: 1300 us -> 1240 us
    pallas_call x1, Pallas kernels: 1300 us -> 1240 us  [device_step(): pl.pallas_call(_kernel, name='two_layers', in_specs=[vmem if a.ndim <= PA...]
where the time goes in v3:
time: 1250 us
  Pallas kernels  1240 us (99%)
    pallas_call x1, Pallas kernels, device_step(): pl.pallas_call(_kernel, name='two_layers', in_specs=[vmem if a.ndim <= PA...  1240 us

profile of v3, /device:TPU:0, one launch (start us, length us, event | category | flops | bytes accessed | tf_op | source)
XLA Modules:
  0.0 1247.7 jit_solution(3303433026353084701)
XLA Ops:
  0.0 1244.3 %two_layers.1 = (bf16[8,32,5120]{2,1,0:T(8,128)(2,1)}, bf16[2,2560,640]{2,1,0:T(8,128)(2,1)}, bf16[2,2560,128]{2,1,0:T(8,128)(2,1)}, bf16[2,2560,128]{2,1,0:T(8,...) custom-call(bf16[8,32,5120]{2,1,0:T(8,128)(2,1)} %x_ref.1, ...), custom_call_target="tpu_custom_call" | custom-call | tf_op jit(solution)/shard_map/two_layers/pallas_call | solution.py:774
  1244.3 3.4 copy.14

commit v4 on v3

--- a/solution.py
+++ b/solution.py
@@ -16,25 +16,30 @@
 LX = 2
 LT = LD + 2 * LX
 LH = 2
-LM = (2, 2)
-GAP = (8, 6)
+LM = (7, 4)
+LAGS_M = ((10, 12, 10, 12), (6, 9, 7, 9))
+LAGS_Y = (4, 6)
+FREE = 8
+EXTRA = (6, 0)
+PAIRED = (False, True)
+GAP = (12, 8)
 SLOTS, CHIPS, CORES, PAIR = 4, 4, 2, 2
 ALIGN, LANES = 16, 128
-SEMS = "442222444444448888444433" + "22888"
-GU, ATTN = 9, 8
-
-CUT_A = (20, 38)
-CUT_B = (22, 16)
+SEMS = "4422224444444488884444" + "22888"
+GU, ATTN = 18, 8
+
+CUT_A = (25, 31)
+CUT_B = (23, 19)
 CUTS = 40
 
-ATTEND = ("01234567--------", "012-3-4-5-6-7-------")
-OWN = ("01234567--------", "--012-3-4-5-6-7-----")
-OTHER = ("--------01234567", "---------0-1-2-34567")
-GU_IN_A = ("0000001111111111", "00010220211000111111")
-GU_IN_B = ("111122", "1011")
-QKV_IN_B = ("000000011010101010101", "")
-O_IN_A = ("", "1211")
-O_IN_B = ("00000000000000000000000012", "")
+ATTEND = ("01234567--------", "01-234-5-6---7--------------")
+OWN = ("01234567--------", "---012-34-5--6-7------------")
+OTHER = ("--------01234567", "---------0--1-2-----3--456-7")
+GU_IN_A = ("2000204222220012", "0201010040310002400022030032")
+GU_IN_B = ("02122021212", "2022")
+QKV_IN_B = ("000000000002000000000101000011200000", "")
+O_IN_A = ("", "03")
+O_IN_B = ("000000000000000000000000011000001011", "")
 F32 = jnp.float32
 BF16 = jnp.bfloat16
 
@@ -49,8 +54,8 @@
     x_ref, ga_ref, gm_ref, cos_ref, sin_ref, wq_ref, wk_ref, wv_ref, wo_ref, wg_ref, wu_ref, wd_ref,
     y_ref, rq, rk, rv, ro, rg, ru, ha, hb, rw, row,
     xbuf, mpeer, hst, hv, pown, psib, rd, t1, t2, rx, ry, rx2, ry2, hown, hrecv, cbuf, sbuf, tmp, ox, xres, mst,
-    zs, zr, gs, gr, ds, dr, xs, xr, ys, yr, x2s, x2r, y2s, y2r, ms, mr, os_, or_, hs, hr, mxs, mxr, wxs, wxr,
-    loc, hvs, wl, oxs, oxr, sa, ra, sb, rb, xrs, xrr,
+    zs, zr, gs, gr, ds, dr, xs, xr, ys, yr, x2s, x2r, y2s, y2r, ms, mr, os_, or_, hs, hr, mxs, mxr,
+    loc, hvs, wl, oxs, oxr, sa, ra, sb, rb, xrs, xrr, wxs, wxr,
 ):
     n_layers = wq_ref.shape[0]
     NB, T, D = x_ref.shape
@@ -256,12 +261,12 @@
 
     def w_send(l):
         cols = lanes((1 - x) * V, V)
-        return send(wo_ref.at[l, :, cols], rw.at[...], wxs.at[0], wxr.at[0], xp)
+        return send(wo_ref.at[l, :, cols], rw.at[l], wxs.at[l, 0], wxr.at[l, 0], xp)
 
     def z_oq(l, rows=slice(None)):
         cols = lanes(x * V, V)
-        return (send(wo_ref.at[l, rows, cols], row.at[0, rows], wxs.at[1], wxr.at[1], zp),
-                send(rw.at[rows], row.at[1, rows], wxs.at[2], wxr.at[2], zp))
+        return (send(wo_ref.at[l, rows, cols], row.at[l, 0, rows], wxs.at[l, 1], wxr.at[l, 1], zp),
+                send(rw.at[l, rows], row.at[l, 1, rows], wxs.at[l, 2], wxr.at[l, 2], zp))
 
     def rs_x2(u):
         i = u % SLOTS
@@ -338,7 +343,7 @@
         i = u % SLOTS
         return send(hown.at[u % (LH + 1)], hrecv.at[i], hs.at[i], hr.at[i], zp)
 
-    for d in (z_q(0), z_k(0), z_v(0), z_o(0)):
+    for d in (z_q(0), z_k(0), z_v(0), z_oq(0)[0] if PAIRED[0] else z_o(0)):
         d.start()
     first = [pltpu.make_async_copy(x_ref, xbuf, wl.at[0])]
     for d in first:
@@ -355,6 +360,11 @@
         return carry
 
     lax.fori_loop(0, NB, first_rows, 0)
+    if PAIRED[0]:
+        w_send(0).start()
+        for b in range(NB):
+            for half in range(PAIR):
+                res_send(b, half).start()
 
     def first_forward(i, carry):
         ag_fwd1(ha.at[0], sa, ra, i, cut_a(0))
@@ -406,27 +416,29 @@
             hst[1] = _norm(mpeer[b], gm_ref[pl.ds(l, 1), :])
             h_store(h, theirs(b), 1).start()
 
-        def forward(b):
-            for j in range(PAIR):
-                ag_fwd1(h, sb, rb, PAIR * b + j, cut)
-
-        def forward_more(b):
-            for j in range(PAIR):
-                ag_fwd2(h, sb, rb, PAIR * b + j, cut)
-
+        own_1, own_2, theirs_1, theirs_2 = LAGS_M[l]
         at(1, send_own)
         at(0, start_own)
         at(wait_m + 1, send_theirs)
         at(wait_m, start_theirs)
-        at(wait_m + LX + 1, forward)
-        at(wait_m + LX + LX + 1, forward_more)
+        at(own_1, lambda b: ag_fwd1(h, sb, rb, own(b), cut))
+        at(theirs_1, lambda b: ag_fwd1(h, sb, rb, theirs(b), cut))
+        at(own_2, lambda b: ag_fwd2(h, sb, rb, own(b), cut))
+        at(theirs_2, lambda b: ag_fwd2(h, sb, rb, theirs(b), cut))
 
     def pass_y(l, s):
         last = l + 1 == n_layers
-
-        @when(within(s, NU), s % PAIR == 1 - z)
+        free = FREE if last else 0
+
+        @when(s >= free, s < NU, s % PAIR == 1 - z)
         def _():
             out_send(half_of(s)).start()
+
+        if last:
+            @pl.when(s == free)
+            def _():
+                for b in range(half_of(free)):
+                    out_send(b).start()
 
         def at(lag, run):
             i = s - lag - 1
@@ -434,25 +446,22 @@
 
         def got(b):
             out_send(b).wait()
-            if last:
-                y_store(b).start()
-                return
             hst[0] = _norm(xbuf[b], ga_ref[pl.ds(l + 1, 1), :])
             h_store(ha.at[l + 1], b, 0).start()
             for half in range(PAIR):
                 res_send(b, half).start()
 
-        at(1, got)
         if not last:
+            at(1, got)
             h, cut = ha.at[l + 1], cut_a(l + 1)
 
             def send_own(b):
                 h_store(h, b, 0).wait()
                 ag_send_own(h, sa, ra, b)
 
-            at(LX, send_own)
-            at(LX + LX, lambda b: ag_fwd1(h, sa, ra, b, cut))
-            at(LX + LX + LX, lambda b: ag_fwd2(h, sa, ra, b, cut))
+            at(2, send_own)
+            at(LAGS_Y[0], lambda b: ag_fwd1(h, sa, ra, b, cut))
+            at(LAGS_Y[1], lambda b: ag_fwd2(h, sa, ra, b, cut))
 
     def add(buf, b, start, low, high):
         for at, part in ((start, low), (start + V, high)):
@@ -482,7 +491,7 @@
         return jnp.where(is_own, b_own, b_oth), u, is_own, is_oth
 
     def a_stages(l, k):
-        if l == 0:
+        if not PAIRED[l]:
             rs_steps(k, NU, finish_m)
             return
 
@@ -516,7 +525,7 @@
         pl.when(ok4)(lambda: ra_m(u4, b4, half4).wait())
 
     def a_sends(l, k):
-        if l == 0:
+        if not PAIRED[l]:
             rs_sends(k, NU)
             return
 
@@ -532,7 +541,7 @@
         pl.when(ok3)(lambda: ra_m(u3, b3, half3).start())
 
     def b_steps(l):
-        return GAP[l] + LH + NU
+        return GAP[l] + LH + NU + EXTRA[l]
 
     def pos_of(r):
         rail = r // (CHIPS * T)
@@ -568,10 +577,11 @@
         loads = [pltpu.make_async_copy(wq_ref.at[l], wa_o.at[:, pl.ds(0, QW)], wl.at[0]),
                  pltpu.make_async_copy(wk_ref.at[l], wa_o.at[:, pl.ds(QW, HD)], wl.at[1]),
                  pltpu.make_async_copy(wv_ref.at[l], wa_o.at[:, pl.ds(QW + HD, HD)], wl.at[2]),
-                 pltpu.make_async_copy(wo_ref.at[l] if l == 0 else wo_ref.at[l, :, my_v],
+                 pltpu.make_async_copy(wo_ref.at[l, :, my_v] if PAIRED[l] else wo_ref.at[l],
                                        w_own.at[0], wl.at[3])]
+        from_x = pltpu.make_async_copy(rw.at[l], w_own.at[1], wl.at[7]) if PAIRED[l] else None
         if l > 0:
-            loads.append(pltpu.make_async_copy(rw, w_own.at[1], wl.at[7]))
+            loads.append(from_x)
         for d in loads:
             d.start()
         ag_load(h, sa, ra, 0)
@@ -598,9 +608,17 @@
             pl.when(ok)(lambda: attend(l, ba, h, wa_o, wa_r, o_all))
             b, u, own, oth = a_unit(l, k)
 
+            if PAIRED[l] and l == 0:
+                @pl.when(k == min(table(OWN[l])))
+                def _():
+                    w_send(l).wait()
+                    z_oq(l)[1].start()
+                    from_x.start()
+                    from_x.wait()
+
             @pl.when(own)
             def _():
-                if l == 0:
+                if not PAIRED[l]:
                     store_product(u, [(o_all[b], w_own.at[0], None)], W)
                 else:
                     o_send(o_all, b).wait()
@@ -608,13 +626,13 @@
 
             @pl.when(k == first_other)
             def _():
-                got = (z_o(l),) if l == 0 else z_oq(l)
+                got = z_oq(l) if PAIRED[l] else (z_o(l),)
                 for d in got:
                     d.wait()
-                if l == 0:
+                if not PAIRED[l]:
                     into = [pltpu.make_async_copy(ro, w_oth.at[0], wl.at[5])]
                 else:
-                    into = [pltpu.make_async_copy(row.at[i], w_oth.at[i], wl.at[5 + i]) for i in range(2)]
+                    into = [pltpu.make_async_copy(row.at[l, i], w_oth.at[i], wl.at[5 + i]) for i in range(2)]
                 for d in into:
                     d.start()
                 for d in into:
@@ -622,17 +640,17 @@
 
             @pl.when(oth)
             def _():
-                if l == 0:
+                if not PAIRED[l]:
                     store_product(u, [(o_all[b], w_oth.at[0], None)], W)
                 else:
                     store_product(u, [(o_all[b], w_oth.at[0], None), (ox[b % (NB - 1)], w_oth.at[1], None)], V)
 
             if l > 0:
-                rs_steps(NU + k, NU, finish_y)
+                rs_steps(NU + EXTRA[l - 1] + k, NU, finish_y)
             a_stages(l, k)
             if l > 0:
-                rs_sends(NU + k, NU)
-            if l > 0:
+                rs_sends(NU + EXTRA[l - 1] + k, NU)
+            if PAIRED[l]:
                 @pl.when(ok)
                 def _():
                     for half in range(2):
@@ -641,7 +659,7 @@
 
             a_sends(l, k)
             if l > 0:
-                pass_y(l - 1, NU + k - LT)
+                pass_y(l - 1, NU + EXTRA[l - 1] + k - LT)
             pass_m(l, k)
 
             parts((O_IN_B[l - 1], O_IN_A[l]), k, functools.partial(z_o_part, l))
@@ -690,7 +708,7 @@
 
             v = k - j0 - LH
 
-            @pl.when(v >= 0)
+            @pl.when(within(v, NU))
             def _():
                 hid_send(v).wait()
                 store_product(v, [(hown[v % (LH + 1)], wd_v, mine_h), (hrecv[v % SLOTS], wd_v, theirs_h)], W)
@@ -724,8 +742,8 @@
         pl.run_scoped(
             functools.partial(loop_a, l),
             pltpu.VMEM((W, QW + 2 * HD), BF16), pltpu.VMEM((W, QW + 2 * HD), BF16),
-            pltpu.VMEM((1, QW, W) if l == 0 else (2, QW, V), BF16),
-            pltpu.VMEM((1, QW, W) if l == 0 else (2, QW, V), BF16), pltpu.VMEM((NB, R, QW), BF16))
+            pltpu.VMEM((2, QW, V) if PAIRED[l] else (1, QW, W), BF16),
+            pltpu.VMEM((2, QW, V) if PAIRED[l] else (1, QW, W), BF16), pltpu.VMEM((NB, R, QW), BF16))
         pl.run_scoped(
             functools.partial(loop_b, l),
             pltpu.VMEM((HB, W), BF16), pltpu.VMEM((HB, W), BF16),
@@ -738,6 +756,9 @@
         return carry
 
     lax.fori_loop(NU, NU + LT + 2, tail, 0)
+    for b in range(NB):
+        out_send(b).wait()
+        y_store(b).start()
     for b in range(NB):
         y_store(b).wait()
 
@@ -768,7 +789,7 @@
                 jnp.swapaxes(w_gate, 1, -1), jnp.swapaxes(w_up, 1, -1), w_down)
         half_rows, plane_rows = (L, HB, W), (CORES, CHIPS, T, D)
         shapes = [x_in.shape, w_q.shape, w_k.shape, w_v.shape, w_o.shape[1:], half_rows, half_rows,
-                  (L, NB) + plane_rows, (L, NU) + plane_rows, (QW, V), (PAIR, QW, V)]
+                  (L, NB) + plane_rows, (L, NU) + plane_rows, (L, QW, V), (L, PAIR, QW, V)]
         unit, hop = (PAIR, PAIR, T, W), (PAIR, T, V)
         in_flight, hidden, tables = LH + 1, (HB, R), (CORES, CHIPS, T, HD)
         outs = pl.pallas_call(
@@ -785,7 +806,8 @@
                 buf(F32, *tables), buf(F32, *tables), buf(F32, CHIPS, CORES, T, HD),
                 buf(BF16, NB - 1, R, QW), buf(BF16, NB, T, W), buf(BF16, in_flight, T, V)]
             + [sems(int(ch)) for ch in SEMS] + [sems(NB, CHIPS + 1), sems(NB, CHIPS + 1), sems(NU, CHIPS + 1),
-                                                sems(NU, CHIPS + 1), sems(NB, PAIR), sems(NB, PAIR)],
+                                                sems(NU, CHIPS + 1), sems(NB, PAIR), sems(NB, PAIR),
+                                                sems(L, PAIR + 1), sems(L, PAIR + 1)],
             compiler_params=pltpu.CompilerParams(
                 collective_id=0, has_side_effects=True, vmem_limit_bytes=67_000_000),
         )(*args)

time: 1250 us -> 1220 us (0.976)
  Pallas kernels: 1240 us -> 1220 us
    pallas_call x1, Pallas kernels: 1240 us -> 1220 us  [device_step(): pl.pallas_call(_kernel, name='two_layers', in_specs=[vmem if a.ndim <= PA...]
where the time goes in v4:
time: 1220 us
  Pallas kernels  1220 us (100%)
    pallas_call x1, Pallas kernels, device_step(): pl.pallas_call(_kernel, name='two_layers', in_specs=[vmem if a.ndim <= PA...  1220 us

profile of v4, /device:TPU:0, one launch (start us, length us, event | category | flops | bytes accessed | tf_op | source)
XLA Modules:
  0.0 1224.6 jit_solution(14063276904209705641)
XLA Ops:
  0.0 1221.2 %two_layers.1 = (bf16[8,32,5120]{2,1,0:T(8,128)(2,1)}, bf16[2,2560,640]{2,1,0:T(8,128)(2,1)}, bf16[2,2560,128]{2,1,0:T(8,128)(2,1)}, bf16[2,2560,128]{2,1,0:T(8,...) custom-call(bf16[8,32,5120]{2,1,0:T(8,128)(2,1)} %x_ref.1, ...), custom_call_target="tpu_custom_call" | custom-call | tf_op jit(solution)/shard_map/two_layers/pallas_call | solution.py:795
  1221.2 3.4 copy.14

commit v5 on v4

--- a/solution.py
+++ b/solution.py
@@ -17,10 +17,10 @@
 LT = LD + 2 * LX
 LH = 2
 LM = (7, 4)
-LAGS_M = ((10, 12, 10, 12), (6, 9, 7, 9))
-LAGS_Y = (4, 6)
-FREE = 8
-EXTRA = (6, 0)
+LAGS_M = ((10, 13, 10, 12), (6, 10, 7, 14))
+LAGS_Y = (4, 7)
+FREE = 6
+EXTRA = (7, 0)
 PAIRED = (False, True)
 GAP = (12, 8)
 SLOTS, CHIPS, CORES, PAIR = 4, 4, 2, 2
@@ -28,18 +28,18 @@
 SEMS = "4422224444444488884444" + "22888"
 GU, ATTN = 18, 8
 
-CUT_A = (25, 31)
-CUT_B = (23, 19)
+CUT_A = (29, 34)
+CUT_B = (20, 19)
 CUTS = 40
 
-ATTEND = ("01234567--------", "01-234-5-6---7--------------")
-OWN = ("01234567--------", "---012-34-5--6-7------------")
-OTHER = ("--------01234567", "---------0--1-2-----3--456-7")
-GU_IN_A = ("2000204222220012", "0201010040310002400022030032")
-GU_IN_B = ("02122021212", "2022")
-QKV_IN_B = ("000000000002000000000101000011200000", "")
-O_IN_A = ("", "03")
-O_IN_B = ("000000000000000000000000011000001011", "")
+ATTEND = ("01234567--------", "0123-4-5--6---7---------------")
+OWN = ("01234567--------", "---01234--5--6--7-------------")
+OTHER = ("--------01234567", "---------0--1--2----3---456--7")
+GU_IN_A = ("2000212321221211", "210002120011200220002023221010")
+GU_IN_B = ("0132101231", "232")
+QKV_IN_B = ("0000000000010100000001000100012010000", "")
+O_IN_A = ("", "000011")
+O_IN_B = ("0000000000000000000000100000110000201", "")
 F32 = jnp.float32
 BF16 = jnp.bfloat16
 
@@ -318,11 +318,10 @@
         def _():
             finish(k - LT, *rs_stage4(k - LT))
 
+    def rs_first(k, n):
+        pl.when(within(k, n))(lambda: rs_d(k).start())
+
     def rs_sends(k, n):
-        @pl.when(jnp.logical_and(k >= 0, k < n))
-        def _():
-            rs_d(k).start()
-
         @pl.when(jnp.logical_and(k >= LD, k < n + LD))
         def _():
             rs_x(k - LD).start()
@@ -524,6 +523,11 @@
         b4, u4, half4, ok4 = at(LT)
         pl.when(ok4)(lambda: ra_m(u4, b4, half4).wait())
 
+    def a_first(l, k):
+        _, u, own, oth = a_unit(l, k)
+        first = ra_d if PAIRED[l] else rs_d
+        pl.when(jnp.logical_or(own, oth))(lambda: first(u).start())
+
     def a_sends(l, k):
         if not PAIRED[l]:
             rs_sends(k, NU)
@@ -533,8 +537,6 @@
             b, u, own, oth = a_unit(l, k - lag)
             return b, u, jnp.where(own, z, 1 - z), jnp.logical_or(own, oth)
 
-        _, u1, _, ok1 = at(0)
-        pl.when(ok1)(lambda: ra_d(u1).start())
         _, u2, _, ok2 = at(LD)
         pl.when(ok2)(lambda: ra_y(u2).start())
         b3, u3, half3, ok3 = at(LD + LX)
@@ -606,6 +608,19 @@
             pl.when(next_ok)(lambda: ag_load(h, sa, ra, bn))
             ba, ok = a_attend(l, k)
             pl.when(ok)(lambda: attend(l, ba, h, wa_o, wa_r, o_all))
+            if l > 0:
+                rs_steps(NU + EXTRA[l - 1] + k, NU, finish_y)
+            a_stages(l, k)
+            if l > 0:
+                rs_sends(NU + EXTRA[l - 1] + k, NU)
+            if PAIRED[l]:
+                @pl.when(ok)
+                def _():
+                    for half in range(2):
+                        res_send(ba, half).wait_send()
+                    o_send(o_all, ba).start()
+
+            a_sends(l, k)
             b, u, own, oth = a_unit(l, k)
 
             if PAIRED[l] and l == 0:
@@ -645,19 +660,7 @@
                 else:
                     store_product(u, [(o_all[b], w_oth.at[0], None), (ox[b % (NB - 1)], w_oth.at[1], None)], V)
 
-            if l > 0:
-                rs_steps(NU + EXTRA[l - 1] + k, NU, finish_y)
-            a_stages(l, k)
-            if l > 0:
-                rs_sends(NU + EXTRA[l - 1] + k, NU)
-            if PAIRED[l]:
-                @pl.when(ok)
-                def _():
-                    for half in range(2):
-                        res_send(ba, half).wait_send()
-                    o_send(o_all, ba).start()
-
-            a_sends(l, k)
+            a_first(l, k)
             if l > 0:
                 pass_y(l - 1, NU + EXTRA[l - 1] + k - LT)
             pass_m(l, k)
@@ -680,14 +683,19 @@
             d.start()
 
         def step(k, carry):
+            @pl.when(k == j0 - 1)
+            def _():
+                z_g(l).wait()
+                more[0].start()
+                for d in loads:
+                    d.wait()
+                more[0].wait()
+
             @pl.when(k == j0)
             def _():
-                for d in (z_g(l), z_u(l)):
-                    d.wait()
-                for d in more:
-                    d.start()
-                for d in loads + more:
-                    d.wait()
+                z_u(l).wait()
+                more[1].start()
+                more[1].wait()
 
             @when(k >= j0 - 1, k < j0 + NU - 1)
             def _():
@@ -707,21 +715,22 @@
                 hown[u % (LH + 1)] = (jax.nn.silu(gate) * up).astype(BF16)
 
             v = k - j0 - LH
+            a_stages(l, a_steps(l) + k)
+            rs_steps(v, NU, finish_y)
+
+            a_sends(l, a_steps(l) + k)
+            rs_sends(v, NU)
 
             @pl.when(within(v, NU))
             def _():
                 hid_send(v).wait()
                 store_product(v, [(hown[v % (LH + 1)], wd_v, mine_h), (hrecv[v % SLOTS], wd_v, theirs_h)], W)
 
-            a_stages(l, a_steps(l) + k)
-            rs_steps(v, NU, finish_y)
-
             @when(k >= j0, k < j0 + NU)
             def _():
                 hid_send(k - j0).start()
 
-            a_sends(l, a_steps(l) + k)
-            rs_sends(v, NU)
+            rs_first(v, NU)
             pass_m(l, a_steps(l) + k)
             pass_y(l, v - LT)
 

time: 1220 us -> 1220 us (level)
  no operation moved by 1% of the time
where the time goes in v5:
time: 1220 us
  Pallas kernels  1220 us (100%)
    pallas_call x1, Pallas kernels, device_step(): pl.pallas_call(_kernel, name='two_layers', in_specs=[vmem if a.ndim <= PA...  1220 us

profile of v5, /device:TPU:0, one launch (start us, length us, event | category | flops | bytes accessed | tf_op | source)
XLA Modules:
  0.0 1221.7 jit_solution(2524204376731750290)
XLA Ops:
  0.0 1218.3 %two_layers.1 = (bf16[8,32,5120]{2,1,0:T(8,128)(2,1)}, bf16[2,2560,640]{2,1,0:T(8,128)(2,1)}, bf16[2,2560,128]{2,1,0:T(8,128)(2,1)}, bf16[2,2560,128]{2,1,0:T(8,...) custom-call(bf16[8,32,5120]{2,1,0:T(8,128)(2,1)} %x_ref.1, ...), custom_call_target="tpu_custom_call" | custom-call | tf_op jit(solution)/shard_map/two_layers/pallas_call | solution.py:804
  1218.3 3.4 copy.14

commit v6 on v5

--- a/solution.py
+++ b/solution.py
@@ -187,14 +187,14 @@
 
     def ag_own(h, s, r, u):
         own = h.at[u, 0, q]
-        return [send(own, own, s.at[u, i], r.at[u, i], dev) for i, dev in enumerate((xp, yp))]
+        return [send(own, own, s.at[u], r.at[u, i], dev) for i, dev in enumerate((xp, yp))]
 
     def ag_fwd(h, s, r, u, cut):
         from_x, from_y = h.at[u, 0, qx, :, pl.ds(0, cut)], h.at[u, 0, qy, :, pl.ds(cut, D - cut)]
-        return [send(from_x, from_x, s.at[u, 2], r.at[u, 2], yp), send(from_y, from_y, s.at[u, 3], r.at[u, 3], xp)]
+        return [send(from_x, from_x, s.at[u], r.at[u, PAIR], yp), send(from_y, from_y, s.at[u], r.at[u, PAIR], xp)]
 
     def ag_sib(h, s, r, u):
-        return send(h.at[u, 0], h.at[u, 1], s.at[u, CHIPS], r.at[u, CHIPS], sp)
+        return send(h.at[u, 0], h.at[u, 1], s.at[u], r.at[u, CHIPS - 1], sp)
 
     def ag_send_own(h, s, r, u):
         for d in ag_own(h, s, r, u):
@@ -206,8 +206,8 @@
             fwd.start()
 
     def ag_fwd2(h, s, r, u, cut):
-        for fwd in ag_fwd(h, s, r, u, cut):
-            fwd.wait_recv()
+        block = h.at[u, 0, qd]
+        send(block, block, s.at[u], r.at[u, PAIR], xp).wait_recv()
         ag_sib(h, s, r, u).start()
 
     def ag_local(h, u):
@@ -219,8 +219,8 @@
 
     def ag_finish(h, s, r, u, cut):
         ag_local(h, u).wait()
-        for d in ag_own(h, s, r, u) + ag_fwd(h, s, r, u, cut) + [ag_sib(h, s, r, u)]:
-            d.wait_send()
+        seven = ha.at[0, pl.ds(0, NB - 1), 0, 0]
+        send(seven, seven, s.at[u], r.at[u, 0], sp).wait_send()
 
     def y_store(b):
         return pltpu.make_async_copy(xbuf.at[b], y_ref.at[b], oxs.at[b])
@@ -814,8 +814,8 @@
                 buf(F32, SLOTS, T, V), buf(F32, SLOTS, T, V), buf(BF16, in_flight, *hidden), buf(BF16, SLOTS, *hidden),
                 buf(F32, *tables), buf(F32, *tables), buf(F32, CHIPS, CORES, T, HD),
                 buf(BF16, NB - 1, R, QW), buf(BF16, NB, T, W), buf(BF16, in_flight, T, V)]
-            + [sems(int(ch)) for ch in SEMS] + [sems(NB, CHIPS + 1), sems(NB, CHIPS + 1), sems(NU, CHIPS + 1),
-                                                sems(NU, CHIPS + 1), sems(NB, PAIR), sems(NB, PAIR),
+            + [sems(int(ch)) for ch in SEMS] + [sems(NB), sems(NB, CHIPS), sems(NU), sems(NU, CHIPS),
+                                                sems(NB, PAIR), sems(NB, PAIR),
                                                 sems(L, PAIR + 1), sems(L, PAIR + 1)],
             compiler_params=pltpu.CompilerParams(
                 collective_id=0, has_side_effects=True, vmem_limit_bytes=67_000_000),

time: 1220 us -> 1220 us (level)
  no operation moved by 1% of the time
where the time goes in v6:
time: 1220 us
  Pallas kernels  1220 us (100%)
    pallas_call x1, Pallas kernels, device_step(): pl.pallas_call(_kernel, name='two_layers', in_specs=[vmem if a.ndim <= PA...  1220 us

profile of v6, /device:TPU:0, one launch (start us, length us, event | category | flops | bytes accessed | tf_op | source)
XLA Modules:
  0.0 1220.7 jit_solution(14747934144272632040)
XLA Ops:
  0.0 1217.2 %two_layers.1 = (bf16[8,32,5120]{2,1,0:T(8,128)(2,1)}, bf16[2,2560,640]{2,1,0:T(8,128)(2,1)}, bf16[2,2560,128]{2,1,0:T(8,128)(2,1)}, bf16[2,2560,128]{2,1,0:T(8,...) custom-call(bf16[8,32,5120]{2,1,0:T(8,128)(2,1)} %x_ref.1, ...), custom_call_target="tpu_custom_call" | custom-call | tf_op jit(solution)/shard_map/two_layers/pallas_call | solution.py:804
  1217.3 3.4 copy.14
